TPU v7x, 128 devices: a whole 4x4x4 slice. The times are simulated.
128 devices in a mesh: patch: 128 (over y, z, x, core).
Axes of the slice: x: 4, y: 4, z: 4, core: 2. Of those that a mesh axis runs over, the one named last changes fastest.
Arguments:
- positions: float32 [3, 262144], P(None, 'patch'), may hold values from -6 to 6
- densities: float32 [3, 262144], P(None, 'patch'), may hold values from -6 to 6
- near_src: int32 [2048, 8], P('patch'), may hold values from 0 to 2047, as said below
- near_count: int32 [2048], P('patch'), may hold values from 1 to 8
- far_slot: int32 [2048, 32], P('patch'), may hold values from 0 to 511
- far_class: int32 [2048, 32], P('patch'), may hold values from 0 to 188
- far_count: int32 [2048], P('patch'), may hold values from 1 to 32
- requests: int32 [128, 128, 4], P('patch'), may hold values from 0 to 15, as said below
- up_basis: bfloat16 [2048, 144, 384], P('patch'), may hold values from -0.3125 to 0.3125
- transfer_table: bfloat16 [189, 20736], replicated, may hold values from -0.5 to 0.5
- down_basis: bfloat16 [2048, 144, 9, 128], P('patch'), may hold values from -0.09375 to 0.09375
Outputs:
- shape_grad: float32 [3, 262144], P(None, 'patch')
Inputs may be any that keep to these rules, and one draw needn't show every extreme that they name: `near_src`: the source leaf of each near-field block is held by the device of its target leaf or by the device just before or after it along patch. `requests`: each row names 4 different leaves of the source device, by their index on that device.
All inputs are finite; a program needn't handle non-finite values.
Results may differ from a plain program's by a relative error of at most 0.0042.
Values may be sent and summed in bfloat16 or wider, within the bound.
No kernel may reach another device: no remote copies, remote signals or barrier semaphores. Data moves between devices by JAX's collectives and lax.ppermute only.
A program may use at most 192 MiB of HBM per device.

v0:
```python
import math

import jax
import jax.numpy as jnp
from jax import lax
from jax.sharding import PartitionSpec as P

KERNEL = 1.0 / (8.0 * math.pi)
BLOB = 0.25


def with_halo(x, sides, width):
    for axis, dim in sides:
        peers, length = (lax.axis_size(axis), x.shape[dim])
        up = [(i, (i + 1) % peers) for i in range(peers - 1)]
        down = [(j, i) for i, j in up]
        last = lax.slice_in_dim(x, length - width, length, axis=dim)
        first = lax.slice_in_dim(x, 0, width, axis=dim)
        before = lax.ppermute(last, axis, up)
        after = lax.ppermute(first, axis, down)
        x = jnp.concatenate([before, x, after], axis=dim)
    return x


def passed_along(x, axis, by):
    peers = lax.axis_size(axis)
    pairs = [(i, i + by) for i in range(peers) if 0 <= i + by < peers]
    return lax.ppermute(x, axis, pairs)


def pair_terms(target, source):
    xt = target[:, :3]
    ft = target[:, 3:]
    xs = source[:, :3]
    fs = source[:, 3:]
    sep = xt[:, :, :, None] - xs[:, :, None, :]
    rho_sq = jnp.sum(sep * sep, axis=1) + BLOB
    inv_one = lax.rsqrt(rho_sq)
    inv_three = inv_one / rho_sq
    inv_five = inv_three / rho_sq
    fa = ft[:, :, :, None]
    fb = fs[:, :, None, :]
    prod_ab = jnp.sum(fa * fb, axis=1)
    prod_ar = jnp.sum(fa * sep, axis=1)
    prod_br = jnp.sum(fb * sep, axis=1)
    first = (fa * prod_br[:, None] + fb * prod_ar[:, None] - prod_ab[:, None] * sep) * inv_three[
        :, None
    ]
    second = 3.0 * (prod_ar * prod_br * inv_five)[:, None] * sep
    return (first - second) * KERNEL


def one_hot(indices, count, dtype):
    return (indices[:, None] == jnp.arange(count, dtype=jnp.int32)[None, :]).astype(dtype)


def select_rows(indices, data):
    flat = data.reshape(data.shape[0], -1)
    picked = jnp.dot(
        one_hot(indices, data.shape[0], jnp.float32), flat, precision=lax.Precision.HIGHEST
    )
    return picked.reshape((indices.shape[0],) + data.shape[1:])


def add_rows(total, indices, values):
    hot = one_hot(indices, total.shape[0], jnp.float32)
    flat = values.reshape(values.shape[0], -1)
    added = jnp.dot(hot.T, flat, precision=lax.Precision.HIGHEST)
    return total + added.reshape(total.shape)


def per_device(
    positions,
    densities,
    near_src,
    near_count,
    far_slot,
    far_class,
    far_count,
    requests,
    up_basis,
    transfer_table,
    down_basis,
):
    leaf_num = near_count.shape[0]
    per_leaf = positions.shape[1] // leaf_num
    width = up_basis.shape[1]
    slot_num = near_src.shape[1]
    far_num = far_slot.shape[1]
    device = lax.axis_index("patch")
    stacked = jnp.concatenate([positions, densities], 0)
    window = with_halo(stacked, (("patch", 1),), stacked.shape[1])
    window = window.reshape(6, 3 * leaf_num, per_leaf).transpose(1, 0, 2)
    local = stacked.reshape(6, leaf_num, per_leaf).transpose(1, 0, 2)
    offset = (device - 1) * leaf_num
    start_state = (
        jnp.zeros((leaf_num, 3, per_leaf), jnp.float32),
        jnp.zeros((3 * leaf_num, 3, per_leaf), jnp.float32),
    )

    def near_step(slot, carry):
        tgt_sum, src_part = carry
        index = near_src[:, slot] - offset
        live = (slot < near_count).astype(jnp.float32)
        terms = pair_terms(local, select_rows(index, window)) * live[:, None, None, None]
        tgt_sum = tgt_sum + jnp.sum(terms, axis=3)
        src_part = add_rows(src_part, index, -jnp.sum(terms, axis=2))
        return (tgt_sum, src_part)

    tgt_sum, src_part = lax.fori_loop(0, slot_num, near_step, start_state)
    near = tgt_sum + src_part[leaf_num : 2 * leaf_num]
    for step_by, piece in ((-1, src_part[:leaf_num]), (1, src_part[2 * leaf_num :])):
        near = near + passed_along(piece, "patch", step_by)
    dens_leaf = local[:, 3:]
    dens_round = dens_leaf.reshape(leaf_num, 3 * per_leaf).astype(jnp.bfloat16)
    moments = jnp.einsum(
        "lrq,lq->lr", up_basis, dens_round, preferred_element_type=jnp.float32
    ).astype(jnp.bfloat16)
    asked = lax.all_to_all(requests[0], "patch", split_axis=0, concat_axis=0, tiled=True)
    replies = moments[asked].reshape(asked.shape[0], asked.shape[1] * width)
    table = lax.all_to_all(replies, "patch", split_axis=0, concat_axis=0, tiled=True).reshape(
        -1, width
    )
    operators = jnp.take(transfer_table, far_class.reshape(-1), axis=0).reshape(
        leaf_num, far_num, width, width
    )
    live_far = (jnp.arange(far_num, dtype=jnp.int32)[None, :] < far_count[:, None]).astype(
        jnp.bfloat16
    )
    sources = (
        jnp.take(table, far_slot.reshape(-1), axis=0).reshape(leaf_num, far_num, width)
        * live_far[:, :, None]
    )
    expansion = jnp.einsum("lsij,lsj->li", operators, sources, preferred_element_type=jnp.float32)
    expansion = expansion.astype(jnp.bfloat16)
    field = jnp.einsum("lr,lrqp->lqp", expansion, down_basis, preferred_element_type=jnp.float32)
    far = jnp.einsum(
        "lcp,lckp->lkp",
        dens_leaf,
        field.reshape(leaf_num, 3, 3, per_leaf),
        precision=lax.Precision.HIGHEST,
    )
    return (near + far).transpose(1, 0, 2).reshape(3, leaf_num * per_leaf)


def solution(mesh):
    placed = (
        P(None, "patch"),
        P(None, "patch"),
        P("patch", None),
        P("patch"),
        P("patch", None),
        P("patch", None),
        P("patch"),
        P("patch", None, None),
        P("patch", None, None),
        P(),
        P("patch", None, None, None),
    )
    return jax.shard_map(
        per_device, mesh=mesh, in_specs=placed, out_specs=P(None, "patch"), check_vma=False
    )
```

profile of v0, /device:TPU:24, one launch (start us, length us, event | category | flops | bytes accessed | tf_op | source)
XLA Modules:
  0.0 239.6 jit_solution(7807876388520252501)
XLA Ops:
  0.9 7.8 %collective-permute-start.1 = (f32[6,2048]{1,0:T(8,128)S(1)}, f32[6,2048]{1,0:T(8,128)S(1)}, u32[]{:S(2)}, u32[]{:S(2)}) collective-permute-start(f32[6,2048]{1,0:T(8,128)S(1)} %get-tuple-element.204), channel_id=1, source_target_pairs={{1,0},{2,1},{3,2},{4,3},{5,4},{6,5},{7,6},{8,7},{9,8},{10,9},{11,1... | collective-permute-start | bytes 147464 | tf_op jit(solution)/shard_map/ppermute | solution.py:20
  8.7 1.9 collective-permute-start
  10.6 1.4 copy.33
  12.0 9.5 %all-to-all-start = ((s32[128,1,4]{2,1,0:T(1,128)}), s32[128,1,4]{2,1,0:T(1,128)S(1)}, u32[]{:S(2)}, u32[]{:S(2)}) async-start(s32[128,1,4]{2,1,0:T(1,128)} %bitcast.9), calls=%async_computation | async-start | bytes 131072 | tf_op jit(solution)/shard_map/all_to_all | solution.py:119
  25.5 40.8 %gather_fusion = bf16[512,20736]{1,0:T(8,128)(2,1)} fusion(bf16[189,20736]{1,0:T(8,128)(2,1)} %param.22, s32[1024]{0:T(1024)S(1)} %pad_clamp_fusion.2), kind=kCustom, calls=%fused_computation | custom fusion | bytes 42469376 | tf_op jit(solution)/shard_map/jit(_take)/gather | solution.py:124
  66.3 67.3 %gather.16 = bf16[16,32,144,144]{3,2,1,0:T(8,128)(2,1)} reshape(bf16[512,20736]{1,0:T(8,128)(2,1)} %gather_fusion) | data formatting | bytes 42467328 | tf_op jit(solution)/shard_map/jit(_take)/gather | solution.py:124
  133.7 2.0 gather_fusion.1
  136.6 1.6 reduce.3
  139.2 9.8 %all-to-all-start.1 = ((bf16[128,2,288]{2,1,0:T(2,128)(2,1)}), bf16[128,2,288]{2,1,0:T(2,128)(2,1)S(1)}, u32[]{:S(2)}, u32[]{:S(2)}) async-start(bf16[128,2,288]{2,1,0:T(2,128)(2,1)} %reshape.271), calls=%async_computation.1 | async-start | bytes 393216 | tf_op jit(solution)/shard_map/all_to_all | solution.py:121
  149.0 56.9 %while.16 = (s32[]{:T(128)}, f32[16,3,128]{2,1,0:T(4,128)S(1)}, f32[48,3,128]{2,0,1:T(8,128)S(1)}, f32[16,6,128]{2,1,0:T(8,128)S(1)}, s32[16,8]{0,1:T(8,128)}, /...) while((s32[]{:T(128)}, f32[16,3,128]{2,1,0:T(4,128)S(1)}, ...), condition=%wide.region_7.0_spmd.clone, body=%wide.region_0.0_spmd.clone.sunk | while | flops 27962928 | bytes 15712836 | solution.py:110
  150.0 2.2 fusion.58
  152.7 3.0 %fusion.59 = (f32[16,3,128]{2,1,0:T(4,128)S(1)}, f32[16,3,128]{2,1,0:T(4,128)S(1)}) fusion(f32[16]{0:T(128)S(1)} %compare_select_fusion.7, f32[16,128,128]{2,1,0:T(8,128)S(1)} %get-tuple-element.276, f32[16,128,128]{2,1,0:T(8,128)S(1)} %get-tuple-element.277, f32[16,128,128]{2,1,0:T(8,128)S(1)} %get-tuple-element.278, ...), kind=kLoop, calls=%fused_computation.16.clone.1 | loop fusion | flops 9424896 | bytes 5390400 | tf_op jit(solution)/shard_map/while/body/eval_jaxpr/reduce_sum | solution.py:107
  157.2 2.2 fusion.58
  159.8 3.0 %fusion.59 = (f32[16,3,128]{2,1,0:T(4,128)S(1)}, f32[16,3,128]{2,1,0:T(4,128)S(1)}) fusion(f32[16]{0:T(128)S(1)} %compare_select_fusion.7, f32[16,128,128]{2,1,0:T(8,128)S(1)} %get-tuple-element.276, f32[16,128,128]{2,1,0:T(8,128)S(1)} %get-tuple-element.277, f32[16,128,128]{2,1,0:T(8,128)S(1)} %get-tuple-element.278, ...), kind=kLoop, calls=%fused_computation.16.clone.1 | loop fusion | flops 9424896 | bytes 5390400 | tf_op jit(solution)/shard_map/while/body/eval_jaxpr/reduce_sum | solution.py:107
  164.3 2.2 fusion.58
  167.0 3.0 %fusion.59 = (f32[16,3,128]{2,1,0:T(4,128)S(1)}, f32[16,3,128]{2,1,0:T(4,128)S(1)}) fusion(f32[16]{0:T(128)S(1)} %compare_select_fusion.7, f32[16,128,128]{2,1,0:T(8,128)S(1)} %get-tuple-element.276, f32[16,128,128]{2,1,0:T(8,128)S(1)} %get-tuple-element.277, f32[16,128,128]{2,1,0:T(8,128)S(1)} %get-tuple-element.278, ...), kind=kLoop, calls=%fused_computation.16.clone.1 | loop fusion | flops 9424896 | bytes 5390400 | tf_op jit(solution)/shard_map/while/body/eval_jaxpr/reduce_sum | solution.py:107
  171.4 2.2 fusion.58
  174.1 3.0 %fusion.59 = (f32[16,3,128]{2,1,0:T(4,128)S(1)}, f32[16,3,128]{2,1,0:T(4,128)S(1)}) fusion(f32[16]{0:T(128)S(1)} %compare_select_fusion.7, f32[16,128,128]{2,1,0:T(8,128)S(1)} %get-tuple-element.276, f32[16,128,128]{2,1,0:T(8,128)S(1)} %get-tuple-element.277, f32[16,128,128]{2,1,0:T(8,128)S(1)} %get-tuple-element.278, ...), kind=kLoop, calls=%fused_computation.16.clone.1 | loop fusion | flops 9424896 | bytes 5390400 | tf_op jit(solution)/shard_map/while/body/eval_jaxpr/reduce_sum | solution.py:107
  178.5 2.2 fusion.58
  181.2 3.0 %fusion.59 = (f32[16,3,128]{2,1,0:T(4,128)S(1)}, f32[16,3,128]{2,1,0:T(4,128)S(1)}) fusion(f32[16]{0:T(128)S(1)} %compare_select_fusion.7, f32[16,128,128]{2,1,0:T(8,128)S(1)} %get-tuple-element.276, f32[16,128,128]{2,1,0:T(8,128)S(1)} %get-tuple-element.277, f32[16,128,128]{2,1,0:T(8,128)S(1)} %get-tuple-element.278, ...), kind=kLoop, calls=%fused_computation.16.clone.1 | loop fusion | flops 9424896 | bytes 5390400 | tf_op jit(solution)/shard_map/while/body/eval_jaxpr/reduce_sum | solution.py:107
  185.6 2.2 fusion.58
  188.3 3.0 %fusion.59 = (f32[16,3,128]{2,1,0:T(4,128)S(1)}, f32[16,3,128]{2,1,0:T(4,128)S(1)}) fusion(f32[16]{0:T(128)S(1)} %compare_select_fusion.7, f32[16,128,128]{2,1,0:T(8,128)S(1)} %get-tuple-element.276, f32[16,128,128]{2,1,0:T(8,128)S(1)} %get-tuple-element.277, f32[16,128,128]{2,1,0:T(8,128)S(1)} %get-tuple-element.278, ...), kind=kLoop, calls=%fused_computation.16.clone.1 | loop fusion | flops 9424896 | bytes 5390400 | tf_op jit(solution)/shard_map/while/body/eval_jaxpr/reduce_sum | solution.py:107
  192.7 2.2 fusion.58
  195.4 3.0 %fusion.59 = (f32[16,3,128]{2,1,0:T(4,128)S(1)}, f32[16,3,128]{2,1,0:T(4,128)S(1)}) fusion(f32[16]{0:T(128)S(1)} %compare_select_fusion.7, f32[16,128,128]{2,1,0:T(8,128)S(1)} %get-tuple-element.276, f32[16,128,128]{2,1,0:T(8,128)S(1)} %get-tuple-element.277, f32[16,128,128]{2,1,0:T(8,128)S(1)} %get-tuple-element.278, ...), kind=kLoop, calls=%fused_computation.16.clone.1 | loop fusion | flops 9424896 | bytes 5390400 | tf_op jit(solution)/shard_map/while/body/eval_jaxpr/reduce_sum | solution.py:107
  199.8 2.2 fusion.58
  202.5 3.0 %fusion.59 = (f32[16,3,128]{2,1,0:T(4,128)S(1)}, f32[16,3,128]{2,1,0:T(4,128)S(1)}) fusion(f32[16]{0:T(128)S(1)} %compare_select_fusion.7, f32[16,128,128]{2,1,0:T(8,128)S(1)} %get-tuple-element.276, f32[16,128,128]{2,1,0:T(8,128)S(1)} %get-tuple-element.277, f32[16,128,128]{2,1,0:T(8,128)S(1)} %get-tuple-element.278, ...), kind=kLoop, calls=%fused_computation.16.clone.1 | loop fusion | flops 9424896 | bytes 5390400 | tf_op jit(solution)/shard_map/while/body/eval_jaxpr/reduce_sum | solution.py:107
  205.9 2.0 collective-permute-start.3
  208.0 7.7 %collective-permute-start.2 = (f32[16,3,128]{2,0,1:T(8,128)S(1)}, f32[16,3,128]{2,0,1:T(8,128)S(1)}, u32[]{:S(2)}, u32[]{:S(2)}) collective-permute-start(f32[16,3,128]{2,0,1:T(8,128)S(1)} %get-tuple-element.202), channel_id=1, source_target_pairs={{1,0},{2,1},{3,2},{4,3},{5,4},{6,5},{7,6},{8,7},{9,8},{10,9},{11,1... | collective-permute-start | bytes 73736 | tf_op jit(solution)/shard_map/ppermute | solution.py:28
  216.0 1.0 reduce.1
  217.3 2.2 gather_fusion.2
  219.7 15.8 %fusion.21 = bf16[16,1,144,1]{2,1,3,0:T(2,128)(2,1)S(1)} fusion(bf16[16,32,144,144]{3,2,1,0:T(8,128)(2,1)} %gather.16, pred[16,32]{1,0:T(8,128)(4,1)S(1)} %compare_and_fusion.1, bf16[16,32,144,1]{2,1,0,3:T(8,128)(2,1)S(1)} %multiply_bitcast_fusion), kind=kOutput, calls=%fused_computation.37 | convolution fusion | flops 31850496 | bytes 21386240 | tf_op jit(solution)/shard_map/lsij,lsj->li/dot_general | solution.py:134
  235.5 3.4 %fusion.29 = f32[16,1,9,128]{3,1,2,0:T(1,128)S(1)} fusion(bf16[16,144,9,128]{3,1,2,0:T(8,128)(2,1)} %param.23, bf16[16,144,1,1]{1,0,2,3:T(8,128)(2,1)S(1)} %bitcast.109), kind=kOutput, calls=%fused_computation.59 | convolution fusion | flops 5308416 | bytes 5386752 | tf_op jit(solution)/shard_map/lr,lrqp->lqp/dot_general | solution.py:136
  (137 shorter events, 22.1 us)
Async XLA Ops:
  0.0 24.7 %copy-start = (bf16[16,144,384]{2,1,0:T(8,128)(2,1)S(1)}, bf16[16,144,384]{2,1,0:T(8,128)(2,1)}, u32[]{:S(2)}) copy-start(bf16[16,144,384]{2,1,0:T(8,128)(2,1)} %param.21) | copy-start | bytes 5308420
  0.9 148.0 %collective-permute-start.1 = (f32[6,2048]{1,0:T(8,128)S(1)}, f32[6,2048]{1,0:T(8,128)S(1)}, u32[]{:S(2)}, u32[]{:S(2)}) collective-permute-start(f32[6,2048]{1,0:T(8,128)S(1)} %get-tuple-element.204), channel_id=1, source_target_pairs={{1,0},{2,1},{3,2},{4,3},{5,4},{6,5},{7,6},{8,7},{9,8},{10,9},{11,1... | collective-permute-start | bytes 147464 | tf_op jit(solution)/shard_map/ppermute | solution.py:20
  8.7 140.2 %collective-permute-start = (f32[6,2048]{1,0:T(8,128)S(1)}, f32[6,2048]{1,0:T(8,128)S(1)}, u32[]{:S(2)}, u32[]{:S(2)}) collective-permute-start(f32[6,2048]{1,0:T(8,128)S(1)} %get-tuple-element.204), channel_id=1, source_target_pairs={{0,1},{1,2},{2,3},{3,4},{4,5},{5,6},{6,7},{7,8},{8,9},{9,10},{10,1... | collective-permute-start | bytes 147464 | tf_op jit(solution)/shard_map/ppermute | solution.py:19
  12.0 121.5 %all-to-all-start = ((s32[128,1,4]{2,1,0:T(1,128)}), s32[128,1,4]{2,1,0:T(1,128)S(1)}, u32[]{:S(2)}, u32[]{:S(2)}) async-start(s32[128,1,4]{2,1,0:T(1,128)} %bitcast.9), calls=%async_computation | async-start | bytes 131072 | tf_op jit(solution)/shard_map/all_to_all | solution.py:119
  133.5 15.4 %copy-start.2 = (f32[3,2048]{1,0:T(4,128)S(1)}, f32[3,2048]{1,0:T(4,128)}, u32[]{:S(2)}) copy-start(f32[3,2048]{1,0:T(4,128)} %param.14) | copy-start | bytes 73732
  133.5 15.4 %copy-start.3 = (f32[3,2048]{1,0:T(4,128)S(1)}, f32[3,2048]{1,0:T(4,128)}, u32[]{:S(2)}) copy-start(f32[3,2048]{1,0:T(4,128)} %param.13) | copy-start | bytes 73732
  133.5 15.5 %copy-start.4 = (s32[16]{0:T(128)S(1)}, s32[16]{0:T(128)}, u32[]{:S(2)}) copy-start(s32[16]{0:T(128)} %param.16) | copy-start | bytes 196
  139.2 76.6 %all-to-all-start.1 = ((bf16[128,2,288]{2,1,0:T(2,128)(2,1)}), bf16[128,2,288]{2,1,0:T(2,128)(2,1)S(1)}, u32[]{:S(2)}, u32[]{:S(2)}) async-start(bf16[128,2,288]{2,1,0:T(2,128)(2,1)} %reshape.271), calls=%async_computation.1 | async-start | bytes 393216 | tf_op jit(solution)/shard_map/all_to_all | solution.py:121
  205.9 33.0 %collective-permute-start.3 = (f32[16,3,128]{2,0,1:T(8,128)S(1)}, f32[16,3,128]{2,0,1:T(8,128)S(1)}, u32[]{:S(2)}, u32[]{:S(2)}) collective-permute-start(f32[16,3,128]{2,0,1:T(8,128)S(1)} %get-tuple-element.203), channel_id=1, source_target_pairs={{0,1},{1,2},{2,3},{3,4},{4,5},{5,6},{6,7},{7,8},{8,9},{9,10},{10,1... | collective-permute-start | bytes 73736 | tf_op jit(solution)/shard_map/ppermute | solution.py:28
  208.0 30.9 %collective-permute-start.2 = (f32[16,3,128]{2,0,1:T(8,128)S(1)}, f32[16,3,128]{2,0,1:T(8,128)S(1)}, u32[]{:S(2)}, u32[]{:S(2)}) collective-permute-start(f32[16,3,128]{2,0,1:T(8,128)S(1)} %get-tuple-element.202), channel_id=1, source_target_pairs={{1,0},{2,1},{3,2},{4,3},{5,4},{6,5},{7,6},{8,7},{9,8},{10,9},{11,1... | collective-permute-start | bytes 73736 | tf_op jit(solution)/shard_map/ppermute | solution.py:28
  219.7 19.9 %copy-start.1 = (bf16[16,144,384]{2,1,0:T(8,128)(2,1)S(1)}, bf16[16,144,384]{2,1,0:T(8,128)(2,1)}, u32[]{:S(2)}) copy-start(bf16[16,144,384]{2,1,0:T(8,128)(2,1)} %param.21) | copy-start | bytes 5308420
where the time goes:
time: 241 us; the launch traced here: 240 us
  local copies, waits for them, and re-layouts  119 us (49%)
  other arithmetic  56.9 us (24%)
  starting transfers between devices  38.8 us (16%)
  matrix products  24 us (10%)
    gather x2, local copies, waits for them, and re-layouts, per_device(): jnp.take(transfer_table, far_class.reshape(-1), axis=0)  108 us
    reduce_sum x8, other arithmetic, near_step(): src_part = add_rows(src_part, index, -jnp.sum(terms, axis=2))  24.2 us
    reduce_sum x8, other arithmetic, pair_terms(): rho_sq = jnp.sum(sep * sep, axis=1) + BLOB  18 us
    dot_general x1, matrix products, per_device(): jnp.einsum('lsij,lsj->li', operators, sources, preferred_element_type=jnp...  15.8 us
    ppermute x2, starting transfers between devices, passed_along(): return lax.ppermute(x, axis, pairs)  9.78 us
    all_to_all x1, starting transfers between devices, per_device(): lax.all_to_all(replies, 'patch', split_axis=0, concat_axis=0, tiled=True)  9.76 us
    all_to_all x1, starting transfers between devices, per_device(): lax.all_to_all(requests[0], 'patch', split_axis=0, concat_axis=0, tiled=T...  9.54 us
    ppermute x1, starting transfers between devices, with_halo(): after = lax.ppermute(first, axis, down)  7.76 us
  transfers between devices with their start and end apart: 6, of which 0 were waited for; matrix products, arithmetic and copies ran while one was open for 82% of the time, Pallas kernels for 0%

commit v1 on v0

v1 whole, which is shorter than its diff:
```python
import functools
import math

import jax
import jax.numpy as jnp
from jax import lax
from jax.experimental import pallas as pl
from jax.experimental.pallas import tpu as pltpu
from jax.sharding import PartitionSpec as P

KERNEL = 1.0 / (8.0 * math.pi)
BLOB = 0.25
LANES = 128
GROUP = 16
F32 = jnp.float32
BF16 = jnp.bfloat16


def iota(shape, dim):
    return lax.broadcasted_iota(jnp.int32, shape, dim)


def moments_body(dens_ref, up_ref, out_ref):
    leaf_num, width, _ = up_ref.shape
    peers = out_ref.shape[0]
    lane = iota((width, LANES), 1)
    cols = jnp.zeros((width, LANES), F32)
    for leaf in range(leaf_num):
        total = None
        for comp in range(3):
            row = dens_ref[comp : comp + 1, leaf * LANES : (leaf + 1) * LANES]
            row = row.astype(BF16).astype(F32)
            part = up_ref[leaf, :, comp * LANES : (comp + 1) * LANES].astype(F32) * row
            total = part if total is None else total + part
        cols = jnp.where(lane == leaf, jnp.sum(total, axis=1, keepdims=True), cols)
    tail = jnp.concatenate([cols[LANES:], jnp.zeros((2 * LANES - width, LANES), F32)], 0)
    rows = jnp.concatenate([cols[:LANES].T[:leaf_num], tail.T[:leaf_num]], 1).astype(BF16)
    out_ref[...] = jnp.broadcast_to(rows[None], (peers,) + rows.shape)


def near_body(src_ref, count_ref, own_ref, left_ref, right_ref, near_ref, to_left_ref, to_right_ref, win, cols, tacc, sacc):
    leaf_num = count_ref.shape[0]
    device = lax.axis_index("patch")
    offset = (device - 1) * leaf_num
    for place, ref in enumerate((left_ref, own_ref, right_ref)):
        for leaf in range(leaf_num):
            win[place * leaf_num + leaf, 0:6] = ref[:, leaf * LANES : (leaf + 1) * LANES]
    sacc[...] = jnp.zeros(sacc.shape, F32)
    lane = iota((LANES, LANES), 1)

    def one_leaf(leaf, _):
        tile = jnp.concatenate([win[leaf_num + leaf], jnp.zeros((LANES - 8, LANES), F32)], 0).T
        for comp in range(6):
            cols[comp] = jnp.broadcast_to(tile[:, comp : comp + 1], (LANES, LANES))
        tacc[...] = jnp.zeros(tacc.shape, F32)

        def one_block(slot, _):
            source = src_ref[leaf, slot] - offset
            row = [jnp.broadcast_to(win[source, comp : comp + 1], (8, LANES)) for comp in range(6)]
            bx = row[3:]
            sums = [jnp.zeros((8, LANES), F32) for _ in range(3)]
            for part in range(LANES // 8):
                at = slice(part * 8, part * 8 + 8)
                ax = [cols[3 + k, at] for k in range(3)]
                sep = [cols[k, at] - row[k] for k in range(3)]
                rho_sq = sep[0] * sep[0] + sep[1] * sep[1] + (sep[2] * sep[2] + BLOB)
                inv_one = lax.rsqrt(rho_sq)
                inv_two = inv_one * inv_one
                inv_three = inv_two * inv_one
                ab = ax[0] * bx[0] + ax[1] * bx[1] + ax[2] * bx[2]
                ar = ax[0] * sep[0] + ax[1] * sep[1] + ax[2] * sep[2]
                br = bx[0] * sep[0] + bx[1] * sep[1] + bx[2] * sep[2]
                coef = (ab + ar * br * (3.0 * inv_two)) * inv_three
                ar = ar * inv_three
                br = br * inv_three
                for k in range(3):
                    term = ax[k] * br + bx[k] * ar - coef * sep[k]
                    tacc[k, at] = tacc[k, at] + term
                    sums[k] = sums[k] + term
            for k in range(3):
                sacc[source, k] = sacc[source, k] + sums[k]
            return 0

        lax.fori_loop(0, count_ref[leaf], one_block, 0)
        flat = jnp.zeros((LANES, LANES), F32)
        for k in range(3):
            flat = jnp.where(lane == k, jnp.sum(tacc[k], axis=1, keepdims=True), flat)
        win[leaf_num + leaf, 6:7] = win[leaf_num + leaf, 6:7]
        cols[0] = flat.T
        spot = pl.ds(pl.multiple_of(leaf * LANES, LANES), LANES)
        near_ref[:, spot] = cols[0, 0:3]
        return 0

    lax.fori_loop(0, leaf_num, one_leaf, 0)
    for place, ref in enumerate((to_left_ref, near_ref, to_right_ref)):
        for leaf in range(leaf_num):
            at = slice(leaf * LANES, (leaf + 1) * LANES)
            part = jnp.sum(sacc[place * leaf_num + leaf], axis=1)
            ref[:, at] = (ref[:, at] - part) * KERNEL if place == 1 else part * -KERNEL


def columns(scratch, value):
    rows, width = value.shape
    scratch[0:rows, 0:width] = value.astype(F32)
    return scratch[...].T


def prep_body(count_ref, slot_ref, class_ref, req_ref, pick_ref, hot_ref, scratch):
    leaf_num, far_num = slot_ref.shape
    cap, peers = req_ref.shape
    scratch[...] = jnp.zeros((LANES, LANES), F32)
    asked = columns(scratch, req_ref[...])
    asked = jnp.concatenate([jnp.broadcast_to(asked[:, t : t + 1], (peers, LANES)) for t in range(cap)], 0)
    asked = asked.astype(BF16)
    slots = columns(scratch, slot_ref[...])
    lane = iota((far_num, LANES), 1)
    for leaf in range(leaf_num):
        at = slice(leaf * far_num, (leaf + 1) * far_num)
        slot = jnp.broadcast_to(slots[:far_num, leaf : leaf + 1], (far_num, LANES)).astype(jnp.int32)
        peer = slot // cap
        key = (slot - peer * cap) * peers + peer - lane
        hots = [jnp.where(key == t * peers, 1.0, 0.0).astype(BF16) for t in range(cap)]
        local = jnp.dot(jnp.concatenate(hots, 1), asked, preferred_element_type=F32)
        key = peer * leaf_num + local.astype(jnp.int32) - lane
        for t in range(pick_ref.shape[1] // LANES):
            pick_ref[at, t * LANES : (t + 1) * LANES] = jnp.where(key == t * LANES, 1.0, 0.0).astype(BF16)
    classes = columns(scratch, class_ref[...])
    row = iota((far_num, LANES), 0)
    for leaf in range(leaf_num):
        at = slice(leaf * far_num, (leaf + 1) * far_num)
        kind = jnp.broadcast_to(classes[:far_num, leaf : leaf + 1], (far_num, LANES)).astype(jnp.int32)
        keep = (lane % leaf_num == leaf) & (row < count_ref[leaf])
        key = jnp.where(keep, kind - lane // leaf_num, -LANES)
        per = LANES // leaf_num
        for t in range(hot_ref.shape[1] // LANES):
            hot_ref[at, t * LANES : (t + 1) * LANES] = jnp.where(key == t * per, 1.0, 0.0).astype(BF16)


def far_body(mom_ref, pick_ref, hot_ref, table, down, dens_ref, near_ref, from_left_ref, from_right_ref, out_ref, pad, sums, tail, last):
    leaf_num, quads, width, _ = down.shape
    classes = table.shape[0]
    groups = pad.shape[0]
    src = jnp.dot(pick_ref[...], mom_ref[...], preferred_element_type=F32)
    src_t = jnp.concatenate([src[:, :LANES].T, src[:, LANES:].T[: width - LANES]], 0).astype(BF16)
    lead = 2 * LANES - width
    cols = GROUP * leaf_num
    for g in range(groups):
        pad[g, 0:lead] = jnp.zeros((lead, cols), BF16)
        pad[g, lead + width :] = jnp.zeros((pad.shape[1] - lead - width, cols), BF16)
        part = jnp.dot(src_t, hot_ref[:, g * cols : (g + 1) * cols], preferred_element_type=F32)
        pad[g, lead : lead + width] = part.astype(BF16)
    keep = classes - classes % 8
    tail[...] = jnp.zeros(tail.shape, F32)
    tail[0 : classes - keep] = table[keep:classes].astype(F32)
    last[0:8] = table[keep - 8 : keep]
    last[8:16] = tail[...].astype(BF16)
    step = width - LANES
    period = LANES // step
    tiles = period + 1
    blocks = width // period
    same = iota((blocks, GROUP, cols), 2) // leaf_num == iota((blocks, GROUP, cols), 1)
    for r in range(period):
        acc = None
        for g in range(groups):
            ref, first = (last, 0) if g == groups - 1 else (table, g * GROUP)
            rows = [ref[first : first + GROUP, (tiles * b + r) * LANES : (tiles * b + r + 2) * LANES] for b in range(blocks)]
            part = jnp.dot(jnp.concatenate(rows, 0), pad[g, lead - step * r : lead - step * r + 2 * LANES], preferred_element_type=F32)
            acc = part if acc is None else acc + part
        acc = jnp.where(same, acc.reshape(blocks, GROUP, cols), 0.0)
        acc = jnp.sum(acc, axis=1)
        for h in range(cols // LANES):
            sums[h, pl.ds(r, blocks, stride=period), :] = acc[:, h * LANES : (h + 1) * LANES]
    fold = jnp.where(iota((leaf_num, cols), 1) % leaf_num == iota((leaf_num, cols), 0), 1.0, 0.0)
    whole = jnp.concatenate([sums[h] for h in range(cols // LANES)], 1)
    expansion = lax.dot_general(fold, whole, (((1,), (1,)), ((), ())), precision=lax.Precision.HIGHEST, preferred_element_type=F32)
    which = iota((leaf_num, width), 0)
    field = [None] * quads
    for leaf in range(leaf_num):
        lhs = jnp.where(which == leaf, expansion, 0.0).astype(BF16)
        for q in range(0, quads, 2):
            both = [down[leaf, i] for i in range(q, min(q + 2, quads))]
            part = jnp.dot(lhs, jnp.concatenate(both, 1), preferred_element_type=F32)
            field[q] = part if field[q] is None else field[q] + part
    quad = [field[q - q % 2][:, (q % 2) * LANES : (q % 2 + 1) * LANES] for q in range(quads)]
    for leaf in range(leaf_num):
        at = slice(leaf * LANES, (leaf + 1) * LANES)
        base = near_ref[:, at] + from_left_ref[:, at] + from_right_ref[:, at]
        far = []
        for k in range(3):
            far.append(sum(dens_ref[c : c + 1, at] * quad[3 * c + k][leaf : leaf + 1] for c in range(3)))
        out_ref[:, at] = base + jnp.concatenate(far, 0)


SMEM = pl.BlockSpec(memory_space=pltpu.SMEM)
VMEM = pl.BlockSpec(memory_space=pltpu.VMEM)


def per_device(positions, densities, near_src, near_count, far_slot, far_class, far_count, requests, up_basis, transfer_table, down_basis):
    leaf_num, slot_num = near_src.shape
    nodes = positions.shape[1]
    width = up_basis.shape[1]
    far_num = far_slot.shape[1]
    peers = requests.shape[1]
    quads = down_basis.shape[2]
    classes = transfer_table.shape[0]
    groups = -(-classes // GROUP)
    own = jnp.concatenate([positions, densities], 0)
    up = [(i, i + 1) for i in range(peers - 1)]
    down = [(j, i) for i, j in up]
    left = lax.ppermute(own, "patch", up)
    right = lax.ppermute(own, "patch", down)
    message = pl.pallas_call(
        moments_body,
        out_shape=jax.ShapeDtypeStruct((peers, leaf_num, 2 * LANES), BF16),
        in_specs=[VMEM, VMEM],
        out_specs=VMEM,
        name="moments",
    )(densities, up_basis)
    table = lax.all_to_all(message, "patch", split_axis=0, concat_axis=0, tiled=True)
    table = table.reshape(peers * leaf_num, 2 * LANES)
    side = jax.ShapeDtypeStruct((3, nodes), F32)
    near, to_left, to_right = pl.pallas_call(
        near_body,
        out_shape=(side, side, side),
        in_specs=[SMEM, SMEM, VMEM, VMEM, VMEM],
        out_specs=(VMEM, VMEM, VMEM),
        scratch_shapes=[
            pltpu.VMEM((3 * leaf_num, 8, LANES), F32),
            pltpu.VMEM((6, LANES, LANES), F32),
            pltpu.VMEM((3, LANES, LANES), F32),
            pltpu.VMEM((3 * leaf_num, 3, 8, LANES), F32),
        ],
        name="near",
    )(near_src, near_count, own, left, right)
    from_right = lax.ppermute(to_left, "patch", down)
    from_left = lax.ppermute(to_right, "patch", up)
    pick, hot = pl.pallas_call(
        prep_body,
        out_shape=(
            jax.ShapeDtypeStruct((leaf_num * far_num, peers * leaf_num), BF16),
            jax.ShapeDtypeStruct((leaf_num * far_num, groups * GROUP * leaf_num), BF16),
        ),
        in_specs=[SMEM, VMEM, VMEM, VMEM],
        out_specs=(VMEM, VMEM),
        scratch_shapes=[pltpu.VMEM((LANES, LANES), F32)],
        name="prep",
    )(far_count, far_slot, far_class, requests[0].T)
    return pl.pallas_call(
        far_body,
        out_shape=side,
        in_specs=[VMEM] * 9,
        out_specs=VMEM,
        scratch_shapes=[
            pltpu.VMEM((groups, 2 * LANES + 2 * LANES - width, GROUP * leaf_num), BF16),
            pltpu.VMEM((GROUP * leaf_num // LANES, width, LANES), F32),
            pltpu.VMEM((8, width * width), F32),
            pltpu.VMEM((GROUP, width * width), BF16),
        ],
        name="far",
    )(table, pick, hot, transfer_table, down_basis.transpose(0, 2, 1, 3), densities, near, from_left, from_right)


def solution(mesh):
    placed = (
        P(None, "patch"),
        P(None, "patch"),
        P("patch", None),
        P("patch"),
        P("patch", None),
        P("patch", None),
        P("patch"),
        P("patch", None, None),
        P("patch", None, None),
        P(),
        P("patch", None, None, None),
    )
    return jax.shard_map(per_device, mesh=mesh, in_specs=placed, out_specs=P(None, "patch"), check_vma=False)
```

time: 241 us -> 81.7 us (0.34)
  local copies, waits for them, and re-layouts: 119 us -> 2.3 us
  other arithmetic: 56.9 us -> 0.02 us
  Pallas kernels: 0 us -> 42.7 us
  matrix products: 24 us -> 0 us
  starting transfers between devices: 38.8 us -> 29.5 us
  waiting for transfers between devices: 0.02 us -> 7.86 us
    gather x4 -> x0, local copies, waits for them, and re-layouts: 112 us -> none  [the longest x2 108 us: per_device(): jnp.take(transfer_table, far_class.reshape(-1), axis=0)]
    pallas_call x0 -> x4, Pallas kernels: none -> 42.7 us  [the longest x1 20.4 us: per_device(): pl.pallas_call(near_body, out_shape=(side, side, side), in_specs=[SMEM, S...]
    reduce_sum x16 -> x0, other arithmetic: 42.2 us -> none  [the longest x8 24.2 us: near_step(): src_part = add_rows(src_part, index, -jnp.sum(terms, axis=2))]
    dot_general x19 -> x0, matrix products: 24 us -> none  [the longest x1 15.8 us: per_device(): jnp.einsum('lsij,lsj->li', operators, sources, preferred_element_type=jnp...]
    all_to_all x2 -> x1, starting transfers between devices: 19.3 us -> 10.3 us  [per_device(): lax.all_to_all(message, 'patch', split_axis=0, concat_axis=0, tiled=True)]
    ppermute x4, waiting for transfers between devices: 0.01 us -> 7.86 us  [the longest x1 6.73 us: per_device(): left = lax.ppermute(own, 'patch', up)]
    eq x8 -> x0, other arithmetic: 5.6 us -> none  [one_hot(): indices[:, None] == jnp.arange(count, dtype=jnp.int32)[None, :]]
    div x8 -> x0, other arithmetic: 3.44 us -> none  [pair_terms(): inv_three = inv_one / rho_sq]
  transfers between devices with their start and end apart: 6 -> 5, of which waited for: 0 -> 2; matrix products, arithmetic and copies ran while one was open for 82% -> 1% of each run, Pallas kernels for 0% -> 30%
where the time goes in v1:
time: 81.7 us; the launch traced here: 82.5 us
  Pallas kernels  42.7 us (52%)
  starting transfers between devices  29.5 us (36%)
  waiting for transfers between devices  7.86 us (10%)
  local copies, waits for them, and re-layouts  2.3 us (3%)
    pallas_call x1, Pallas kernels, per_device(): pl.pallas_call(near_body, out_shape=(side, side, side), in_specs=[SMEM, S...  20.4 us
    pallas_call x1, Pallas kernels, per_device(): pl.pallas_call(far_body, out_shape=side, in_specs=[VMEM] * 9, out_specs=V...  14.5 us
    all_to_all x1, starting transfers between devices, per_device(): lax.all_to_all(message, 'patch', split_axis=0, concat_axis=0, tiled=True)  10.3 us
    ppermute x1, starting transfers between devices, per_device(): from_right = lax.ppermute(to_left, 'patch', down)  7.86 us
    ppermute x1, starting transfers between devices, per_device(): right = lax.ppermute(own, 'patch', down)  7.5 us
    ppermute x1, waiting for transfers between devices, per_device(): left = lax.ppermute(own, 'patch', up)  6.73 us
    pallas_call x1, Pallas kernels, per_device(): pl.pallas_call(prep_body, out_shape=(jax.ShapeDtypeStruct((leaf_num * far...  4.7 us
    pallas_call x1, Pallas kernels, per_device(): pl.pallas_call(moments_body, out_shape=jax.ShapeDtypeStruct((peers, leaf_...  3.08 us
  transfers between devices with their start and end apart: 5, of which 2 were waited for; matrix products, arithmetic and copies ran while one was open for 1% of the time, Pallas kernels for 30%

profile of v1, /device:TPU:24, one launch (start us, length us, event | category | flops | bytes accessed | tf_op | source)
XLA Modules:
  0.0 82.5 jit_solution(13351009286044202999)
XLA Ops:
  0.0 0.0 copy-start.1
  0.0 0.0 copy-start.7
  0.0 0.0 copy-start.8
  0.0 3.1 %moments.1 = bf16[128,16,256]{2,1,0:T(8,128)(2,1)} custom-call(f32[3,2048]{1,0:T(4,128)} %dens_ref.3, bf16[16,144,384]{2,1,0:T(8,128)(2,1)} %up_ref.1), custom_call_target="tpu_custom_call" | custom-call | tf_op jit(solution)/shard_map/moments/pallas_call | solution.py:212
  3.1 10.3 %all-to-all-start = ((bf16[128,16,256]{2,1,0:T(8,128)(2,1)}), bf16[128,16,256]{2,1,0:T(8,128)(2,1)S(1)}, u32[]{:S(2)}, u32[]{:S(2)}) async-start(bf16[128,16,256]{2,1,0:T(8,128)(2,1)} %moments.1), calls=%async_computation | async-start | bytes 2097152 | tf_op jit(solution)/shard_map/all_to_all | solution.py:219
  13.4 0.0 copy-done.1
  13.4 0.0 copy-done.7
  13.4 0.0 copy-start.2
  13.4 7.5 %collective-permute-start.1 = (f32[6,2048]{1,0:T(8,128)S(1)}, f32[6,2048]{1,0:T(8,128)S(1)}, u32[]{:S(2)}, u32[]{:S(2)}) collective-permute-start(f32[6,2048]{1,0:T(8,128)S(1)} %pad_maximum_fusion.own_ref), channel_id=1, source_target_pairs={{1,0},{2,1},{3,2},{4,3},{5,4},{6,5},{7,6},{8,7},{9,8},{10,9},{11,1... | collective-permute-start | bytes 147464 | tf_op jit(solution)/shard_map/ppermute | solution.py:211
  20.9 1.9 %collective-permute-start = (f32[6,2048]{1,0:T(8,128)S(1)}, f32[6,2048]{1,0:T(8,128)S(1)}, u32[]{:S(2)}, u32[]{:S(2)}) collective-permute-start(f32[6,2048]{1,0:T(8,128)S(1)} %pad_maximum_fusion.own_ref), channel_id=1, source_target_pairs={{0,1},{1,2},{2,3},{3,4},{4,5},{5,6},{6,7},{7,8},{8,9},{9,10},{10,1... | collective-permute-start | bytes 147464 | tf_op jit(solution)/shard_map/ppermute | solution.py:210
  22.9 0.0 copy-done.8
  22.9 0.7 copy.12.src_ref
  23.5 1.1 %collective-permute-done.1.right_ref = f32[6,2048]{1,0:T(8,128)S(1)} collective-permute-done((f32[6,2048]{1,0:T(8,128)S(1)}, f32[6,2048]{1,0:T(8,128)S(1)}, u32[]{:S(2)}, u32[]{:S(2)}) %collective-permute-start.1) | collective-permute-done | bytes 49184 | tf_op jit(solution)/shard_map/ppermute | solution.py:211
  24.7 0.0 copy-start.3
  24.7 6.7 %collective-permute-done.left_ref = f32[6,2048]{1,0:T(8,128)S(1)} collective-permute-done((f32[6,2048]{1,0:T(8,128)S(1)}, f32[6,2048]{1,0:T(8,128)S(1)}, u32[]{:S(2)}, u32[]{:S(2)}) %collective-permute-start) | collective-permute-done | bytes 49184 | tf_op jit(solution)/shard_map/ppermute | solution.py:210
  31.4 0.0 copy-done.2
  31.4 0.0 copy-done.3
  31.4 0.0 copy-start.4
  31.4 0.6 copy-done.4
  32.0 20.4 %near.1 = (f32[3,2048]{1,0:T(4,128)}, f32[3,2048]{1,0:T(4,128)}, f32[3,2048]{1,0:T(4,128)}) custom-call(s32[16,8]{1,0:T(8,128)} %copy.12.src_ref, s32[16]{0:T(128)} %count_ref.3, f32[6,2048]{1,0:T(8,128)} %copy-done.2, f32[6,2048]{1,0:T(8,128)} %copy-done.4, f32[6,2048]{1,0:T(8,128)} %copy-done.3), custom_call_target="tpu_custom_call" | custom-call | tf_op jit(solution)/shard_map/near/pallas_call | solution.py:222
  52.4 1.9 %collective-permute-start.2 = (f32[3,2048]{1,0:T(4,128)}, f32[3,2048]{1,0:T(4,128)S(1)}, u32[]{:S(2)}, u32[]{:S(2)}) collective-permute-start(f32[3,2048]{1,0:T(4,128)} %get-tuple-element.13), channel_id=1, source_target_pairs={{0,1},{1,2},{2,3},{3,4},{4,5},{5,6},{6,7},{7,8},{8,9},{9,10},{10,1... | collective-permute-start | bytes 73736 | tf_op jit(solution)/shard_map/ppermute | solution.py:236
  54.3 7.9 %collective-permute-start.3 = (f32[3,2048]{1,0:T(4,128)}, f32[3,2048]{1,0:T(4,128)S(1)}, u32[]{:S(2)}, u32[]{:S(2)}) collective-permute-start(f32[3,2048]{1,0:T(4,128)} %get-tuple-element.14), channel_id=1, source_target_pairs={{1,0},{2,1},{3,2},{4,3},{5,4},{6,5},{7,6},{8,7},{9,8},{10,9},{11,1... | collective-permute-start | bytes 73736 | tf_op jit(solution)/shard_map/ppermute | solution.py:235
  62.2 4.7 %prep.1 = (bf16[512,2048]{1,0:T(8,128)(2,1)}, bf16[512,3072]{1,0:T(8,128)(2,1)}) custom-call(s32[16]{0:T(128)} %count_ref.2, s32[16,32]{1,0:T(8,128)} %slot_ref.1, s32[16,32]{1,0:T(8,128)} %class_ref.1, s32[4,128]{1,0:T(4,128)} %bitcast.7), custom_call_target="tpu_custom_call" | custom-call | tf_op jit(solution)/shard_map/prep/pallas_call | solution.py:237
  66.9 0.0 collective-permute-done.2.from_left_ref
  66.9 0.0 collective-permute-done.3.from_right_ref
  66.9 0.0 copy-start.6
  66.9 0.0 all-to-all-done
  66.9 0.0 copy-start
  67.0 0.6 copy-done.5
  67.5 0.0 copy-done.6
  67.5 0.4 copy-done
  68.0 14.5 %far.1 = f32[3,2048]{1,0:T(4,128)} custom-call(bf16[2048,256]{1,0:T(8,128)(2,1)} %bitcast.6, bf16[512,2048]{1,0:T(8,128)(2,1)} %get-tuple-element.10.pick_ref, bf16[512,3072]{1,0:T(8,128)(2,1)} %get-tuple-element.11.hot_ref, bf16[189,20736]{1,0:T(8,128)(2,1)} %table.1, bf16[16,9,144,128]{3,2,1,0:T(8,128)(2,1)} %bitcast.5, f32[3,2048]{1,0:T(4,128)} %dens_ref.3, ...), custom_call_target="tpu_custom_call" | custom-call | tf_op jit(solution)/shard_map/far/pallas_call | solution.py:248
  (2 shorter events, 0.0 us)
Async XLA Ops:
  0.0 13.4 %copy-start.1 = (f32[3,2048]{1,0:T(4,128)S(1)}, f32[3,2048]{1,0:T(4,128)}, u32[]{:S(2)}) copy-start(f32[3,2048]{1,0:T(4,128)} %dens_ref.3) | copy-start | bytes 73732
  0.0 13.4 %copy-start.7 = (f32[3,2048]{1,0:T(4,128)S(1)}, f32[3,2048]{1,0:T(4,128)}, u32[]{:S(2)}) copy-start(f32[3,2048]{1,0:T(4,128)} %param.11) | copy-start | bytes 73732
  0.0 22.9 %copy-start.8 = (s32[16,8]{0,1:T(8,128)S(1)}, s32[16,8]{0,1:T(8,128)}, u32[]{:S(2)}) copy-start(s32[16,8]{0,1:T(8,128)} %param.13) | copy-start | bytes 1540
  3.1 63.8 %all-to-all-start = ((bf16[128,16,256]{2,1,0:T(8,128)(2,1)}), bf16[128,16,256]{2,1,0:T(8,128)(2,1)S(1)}, u32[]{:S(2)}, u32[]{:S(2)}) async-start(bf16[128,16,256]{2,1,0:T(8,128)(2,1)} %moments.1), calls=%async_computation | async-start | bytes 2097152 | tf_op jit(solution)/shard_map/all_to_all | solution.py:219
  13.4 18.0 %copy-start.2 = (f32[6,2048]{1,0:T(8,128)}, f32[6,2048]{1,0:T(8,128)S(1)}, u32[]{:S(2)}) copy-start(f32[6,2048]{1,0:T(8,128)S(1)} %pad_maximum_fusion.own_ref) | copy-start | bytes 147460
  13.4 11.2 %collective-permute-start.1 = (f32[6,2048]{1,0:T(8,128)S(1)}, f32[6,2048]{1,0:T(8,128)S(1)}, u32[]{:S(2)}, u32[]{:S(2)}) collective-permute-start(f32[6,2048]{1,0:T(8,128)S(1)} %pad_maximum_fusion.own_ref), channel_id=1, source_target_pairs={{1,0},{2,1},{3,2},{4,3},{5,4},{6,5},{7,6},{8,7},{9,8},{10,9},{11,1... | collective-permute-start | bytes 147464 | tf_op jit(solution)/shard_map/ppermute | solution.py:211
  20.9 10.5 %collective-permute-start = (f32[6,2048]{1,0:T(8,128)S(1)}, f32[6,2048]{1,0:T(8,128)S(1)}, u32[]{:S(2)}, u32[]{:S(2)}) collective-permute-start(f32[6,2048]{1,0:T(8,128)S(1)} %pad_maximum_fusion.own_ref), channel_id=1, source_target_pairs={{0,1},{1,2},{2,3},{3,4},{4,5},{5,6},{6,7},{7,8},{8,9},{9,10},{10,1... | collective-permute-start | bytes 147464 | tf_op jit(solution)/shard_map/ppermute | solution.py:210
  24.7 6.7 %copy-start.3 = (f32[6,2048]{1,0:T(8,128)}, f32[6,2048]{1,0:T(8,128)S(1)}, u32[]{:S(2)}) copy-start(f32[6,2048]{1,0:T(8,128)S(1)} %collective-permute-done.1.right_ref) | copy-start | bytes 147460
  31.4 0.6 copy-start.4
  52.4 14.5 %collective-permute-start.2 = (f32[3,2048]{1,0:T(4,128)}, f32[3,2048]{1,0:T(4,128)S(1)}, u32[]{:S(2)}, u32[]{:S(2)}) collective-permute-start(f32[3,2048]{1,0:T(4,128)} %get-tuple-element.13), channel_id=1, source_target_pairs={{0,1},{1,2},{2,3},{3,4},{4,5},{5,6},{6,7},{7,8},{8,9},{9,10},{10,1... | collective-permute-start | bytes 73736 | tf_op jit(solution)/shard_map/ppermute | solution.py:236
  54.3 12.6 %collective-permute-start.3 = (f32[3,2048]{1,0:T(4,128)}, f32[3,2048]{1,0:T(4,128)S(1)}, u32[]{:S(2)}, u32[]{:S(2)}) collective-permute-start(f32[3,2048]{1,0:T(4,128)} %get-tuple-element.14), channel_id=1, source_target_pairs={{1,0},{2,1},{3,2},{4,3},{5,4},{6,5},{7,6},{8,7},{9,8},{10,9},{11,1... | collective-permute-start | bytes 73736 | tf_op jit(solution)/shard_map/ppermute | solution.py:235
  66.9 0.6 copy-start.5
  66.9 0.6 copy-start.6
  66.9 1.0 %copy-start = (bf16[128,16,256]{2,1,0:T(8,128)(2,1)}, bf16[128,16,256]{2,1,0:T(8,128)(2,1)S(1)}, u32[]{:S(2)}) copy-start(bf16[128,16,256]{2,1,0:T(8,128)(2,1)S(1)} %all-to-all-done) | copy-start | bytes 3145732

commit v2 on v1

v2 whole, which is shorter than its diff:
```python
import math

import jax
import jax.numpy as jnp
from jax import lax
from jax.experimental import pallas as pl
from jax.experimental.pallas import tpu as pltpu
from jax.sharding import PartitionSpec as P


KERNEL = 1.0 / (8.0 * math.pi)
BLOB = 0.25
LANES = 128
GROUP = 16
F32 = jnp.float32
BF16 = jnp.bfloat16


def iota(shape, dim):
    return lax.broadcasted_iota(jnp.int32, shape, dim)


def front_body(pos_hbm, dens_hbm, src_hbm, count_hbm, up_hbm, own_ref, out_ref, pos_ref, dens_ref, src_ref, count_ref, up_ref, sem):
    refs = ((pos_hbm, pos_ref), (dens_hbm, dens_ref), (src_hbm, src_ref), (count_hbm, count_ref), (up_hbm, up_ref))
    copies = [pltpu.make_async_copy(a, b, sem.at[i]) for i, (a, b) in enumerate(refs)]
    for copy in copies:
        copy.start()
    leaf_num, width, _ = up_ref.shape
    nodes = pos_ref.shape[1]
    slots = src_ref.shape[0]
    own_ref[6:, :nodes] = jnp.zeros((2, nodes), F32)
    own_ref[:, nodes:] = jnp.zeros((slots, LANES), F32)
    for copy in copies[:4]:
        copy.wait()
    own_ref[0:3, :nodes] = pos_ref[...]
    own_ref[3:6, :nodes] = dens_ref[...]
    live = iota((slots, leaf_num), 0) < count_ref[...]
    own_ref[:, nodes : nodes + leaf_num] = jnp.where(live, src_ref[...] + 1, 0).astype(F32)
    copies[4].wait()
    lane = iota((width, LANES), 1)
    cols = jnp.zeros((width, LANES), F32)
    for leaf in range(leaf_num):
        total = None
        for comp in range(3):
            row = dens_ref[comp : comp + 1, leaf * LANES : (leaf + 1) * LANES]
            row = row.astype(BF16).astype(F32)
            part = up_ref[leaf, :, comp * LANES : (comp + 1) * LANES].astype(F32) * row
            total = part if total is None else total + part
        cols = jnp.where(lane == leaf, jnp.sum(total, axis=1, keepdims=True), cols)
    step = width - LANES
    reps = LANES // step
    tails = jnp.concatenate([cols[LANES:]] * reps, 0).T[:leaf_num]
    tails = jnp.where(iota(tails.shape, 1) // step == iota(tails.shape, 0) % reps, tails, 0.0)
    tails = [jnp.sum(tails[i : i + reps], axis=0, keepdims=True) for i in range(0, leaf_num, reps)]
    rows = jnp.concatenate([cols[:LANES].T[:leaf_num]] + tails, 0)
    rows = jnp.concatenate([rows] * 8, 0).astype(BF16)
    for i in range(out_ref.shape[0] // rows.shape[0]):
        out_ref[i * rows.shape[0] : (i + 1) * rows.shape[0]] = rows


def split(x):
    high = x.astype(BF16).astype(F32)
    mid = (x - high).astype(BF16).astype(F32)
    low = (x - high - mid).astype(BF16).astype(F32)
    return high, mid, low


TARGET_PARTS = (0, 0, 1, 0, 2, 1)
SOURCE_PARTS = (0, 1, 0, 2, 0, 1)


def target_rows(tile):
    row = iota(tile.shape, 0)
    x = jnp.where(row < 3, tile, 0.0)
    f = jnp.where(row < 3, pltpu.roll(tile, 5, 0), 0.0)
    norm = jnp.sum(x * x, axis=0, keepdims=True) + BLOB
    cross = jnp.sum(x * f, axis=0, keepdims=True)
    parts, norms, crosses = split(tile), split(norm), split(cross)
    out = []
    for q in range(6):
        extra = norms[q] if q < 3 else crosses[q - 3]
        out.append(jnp.where(row < 6, parts[TARGET_PARTS[q]], jnp.where(row == 6, extra, 1.0 if q < 3 else 0.0)))
    return jnp.concatenate(out, 0)


def source_rows(tile):
    row = iota(tile.shape, 0)
    first, second = row < 3, (row >= 3) & (row < 6)
    x = jnp.where(first, tile, 0.0)
    f = jnp.where(first, pltpu.roll(tile, 5, 0), 0.0)
    norms = split(jnp.sum(x * x, axis=0, keepdims=True))
    crosses = split(-3.0 * jnp.sum(x * f, axis=0, keepdims=True))
    parts = split(tile)
    low = split(pltpu.roll(tile, 3, 0))
    triple = split(3.0 * f)
    rho, ab, ar, br = [], [], [], []
    for q in range(6):
        k = SOURCE_PARTS[q]
        main = jnp.where(first, -2.0 * parts[k], 0.0)
        if q < 3:
            main = jnp.where(row == 6, 1.0, jnp.where(row == 7, norms[q], main))
        rho.append(main)
        ab.append(jnp.where(second, parts[k], 0.0))
        ar.append(jnp.where(second, -low[k], jnp.where(row == 6, 0.0 if q < 3 else 1.0, 0.0)))
        br.append(jnp.where(first, triple[k], jnp.where(row == 7, crosses[q], 0.0) if q < 3 else 0.0))
    return [jnp.concatenate(rows, 0).astype(BF16) for rows in (rho, ab, ar, br)]


def middle_body(own_ref, left_ref, right_ref, count_ref, slot_ref, class_ref, req_ref, near_ref, main_ref, tail_ref, code_ref, kind_ref, win, lhs, rhs, acc, one, two, list_v, list_s, pairs, sem, flip):
    near_terms(own_ref, left_ref, right_ref, near_ref, win, lhs, rhs, acc, one, two, list_v, list_s, pairs, sem)
    select_terms(count_ref, slot_ref, class_ref, req_ref, main_ref, tail_ref, code_ref, kind_ref, flip)


def near_terms(own_ref, left_ref, right_ref, near_ref, win, lhs, rhs, acc, one, two, list_v, list_s, pairs, sem):
    leaf_num = acc.shape[0] - 1
    nodes = leaf_num * LANES
    slots = list_v.shape[1]
    device = lax.axis_index("patch")
    offset = (device - 1) * leaf_num + 1
    halo = (left_ref, own_ref, right_ref)
    for place, ref in enumerate(halo):
        list_v[place] = ref[:, nodes:].astype(jnp.int32)
    copy = pltpu.make_async_copy(list_v, list_s, sem)
    copy.start()
    acc[...] = jnp.zeros(acc.shape, F32)
    for place, ref in enumerate(halo):
        for leaf in range(leaf_num):
            tile = ref[:, leaf * LANES : (leaf + 1) * LANES]
            win[place * leaf_num + leaf] = tile
            for k, rows in enumerate(source_rows(tile)):
                rhs[place * leaf_num + leaf, :, k * LANES : (k + 1) * LANES] = rows
            if place == 1:
                lhs[leaf] = target_rows(tile).T.astype(BF16)
    lhs[leaf_num] = jnp.zeros(lhs.shape[1:], BF16)
    copy.wait()
    count = 0
    for place in range(3):
        def scan(leaf, count):
            for slot in range(slots):
                listed = list_s[place, slot, leaf]
                source = listed - offset
                mine = (listed > 0) & (source >= leaf_num) & (source < 2 * leaf_num)
                pairs[count] = (source - leaf_num) * 64 + (place * leaf_num + leaf)
                count = count + mine.astype(jnp.int32)
                if place == 1:
                    pairs[count] = leaf * 64 + source
                    count = count + (listed > 0).astype(jnp.int32)
            return count

        count = lax.fori_loop(0, leaf_num, scan, count)
    for i in range(3):
        pairs[count + i] = leaf_num * 64

    def products(at, buf):
        pair = pairs[at]
        buf[...] = jnp.dot(lhs[pair // 64], rhs[pair % 64], preferred_element_type=F32)

    def add_terms(at, buf):
        pair = pairs[at]
        target, source = pair // 64, pair % 64
        row = [jnp.broadcast_to(win[source, k : k + 1], (8, LANES)) for k in range(6)]
        for part in range(LANES // 8):
            i = slice(part * 8, part * 8 + 8)
            rho_sq, ab, ar, br = [buf[i, k * LANES : (k + 1) * LANES] for k in range(4)]
            inv_one = lax.rsqrt(rho_sq)
            inv_two = inv_one * inv_one
            inv_three = inv_two * inv_one
            coef = (ab + ar * br * inv_two) * inv_three
            ar = ar * inv_three
            acc[target, 0, i] += br * inv_three
            acc[target, 1, i] += coef
            for k in range(3):
                acc[target, 2 + k, i] += row[3 + k] * ar + row[k] * coef

    products(0, one)

    def two_blocks(step, _):
        products(2 * step + 1, two)
        add_terms(2 * step, one)
        products(2 * step + 2, one)
        add_terms(2 * step + 1, two)
        return 0

    lax.fori_loop(0, (count + 1) // 2, two_blocks, 0)
    lane = iota((LANES, LANES), 1)
    for leaf in range(leaf_num):
        flat = jnp.zeros((LANES, LANES), F32)
        for k in range(5):
            flat = jnp.where(lane == k, jnp.sum(acc[leaf, k], axis=1, keepdims=True), flat)
        flat = flat.T
        tile = win[leaf_num + leaf]
        total = flat[0:1] * tile[3:6] * (1.0 / 3.0) + flat[2:5] - flat[1:2] * tile[0:3]
        near_ref[:, leaf * LANES : (leaf + 1) * LANES] = total * KERNEL


def columns(scratch, value):
    rows, width = value.shape
    scratch[0:rows, 0:width] = value.astype(F32)
    return scratch[...].T


def select_terms(count_ref, slot_ref, class_ref, req_ref, main_ref, tail_ref, code_ref, kind_ref, scratch):
    leaf_num, far_num = slot_ref.shape
    cap, peers = req_ref.shape
    reps = LANES // leaf_num
    half = peers // 2
    rows = main_ref.shape[1] // half
    scratch[...] = jnp.zeros((LANES, LANES), F32)
    asked = columns(scratch, req_ref[...])
    asked = jnp.concatenate([jnp.broadcast_to(asked[:, t : t + 1], (peers, LANES)) for t in range(cap)], 0)
    asked = asked.astype(BF16)
    slots = columns(scratch, slot_ref[...])
    classes = columns(scratch, class_ref[...])
    lane = iota((far_num, LANES), 1)
    row = iota((far_num, LANES), 0)

    def hots(ref, at, key, stride):
        for t in range(ref.shape[1] // LANES):
            ref[at, t * LANES : (t + 1) * LANES] = jnp.where(key == t * stride, 1.0, 0.0).astype(BF16)

    for leaf in range(leaf_num):
        at = slice(leaf * far_num, (leaf + 1) * far_num)
        slot = jnp.broadcast_to(slots[:far_num, leaf : leaf + 1], (far_num, LANES)).astype(jnp.int32)
        peer = slot // cap
        key = (slot - peer * cap) * peers + peer - lane
        picks = [jnp.where(key == t * peers, 1.0, 0.0).astype(BF16) for t in range(cap)]
        local = jnp.dot(jnp.concatenate(picks, 1), asked, preferred_element_type=F32).astype(jnp.int32)
        upper = (peer >= half).astype(jnp.int32)
        base = (peer - upper * half) * rows - lane
        hots(main_ref, at, base + local, LANES)
        hots(tail_ref, at, base + leaf_num + local // reps, LANES)
        code_ref[at] = (upper + 2 * (lane // leaf_num == local % reps).astype(jnp.int32)).astype(BF16)
        kind = jnp.broadcast_to(classes[:far_num, leaf : leaf + 1], (far_num, LANES)).astype(jnp.int32)
        keep = (lane % leaf_num == leaf) & (row < count_ref[leaf])
        kind_ref[at] = jnp.where(keep, kind - lane // leaf_num, -LANES).astype(BF16)


def far_body(mom_ref, main_ref, tail_ref, code_ref, kind_ref, own_ref, near_ref, table_hbm, down_hbm, out_ref, table, down, pad, sums, tail, last, sem):
    fetch = pltpu.make_async_copy(table_hbm, table, sem.at[0])
    fetch_down = pltpu.make_async_copy(down_hbm, down, sem.at[1])
    fetch.start()
    fetch_down.start()
    leaf_num, quads, width, _ = down.shape
    classes = table.shape[0]
    groups = pad.shape[0]
    half = mom_ref.shape[0] // 2
    both = jnp.concatenate([mom_ref[:half], mom_ref[half:]], 1)
    main = jnp.dot(main_ref[...], both, preferred_element_type=F32)
    tails = jnp.dot(tail_ref[...], both, preferred_element_type=F32)
    code = code_ref[...].astype(F32)
    upper = (code == 1.0) | (code == 3.0)
    main = jnp.where(upper, main[:, LANES:], main[:, :LANES]).T
    tails = jnp.where(upper, tails[:, LANES:], tails[:, :LANES])
    tails = jnp.where(code >= 2, tails, 0.0).T
    extra = width - LANES
    tails = sum(tails[i * extra : (i + 1) * extra] for i in range(LANES // extra))
    src_t = jnp.concatenate([main, tails], 0).astype(BF16)
    kind = kind_ref[...]
    one, zero = jnp.ones((), BF16), jnp.zeros((), BF16)
    lead = 2 * LANES - width
    cols = GROUP * leaf_num
    for g in range(groups):
        pad[g, 0:lead] = jnp.zeros((lead, cols), BF16)
        pad[g, lead + width :] = jnp.zeros((pad.shape[1] - lead - width, cols), BF16)
        hot = [jnp.where(kind == (g * (cols // LANES) + h) * (LANES // leaf_num), one, zero) for h in range(cols // LANES)]
        part = jnp.dot(src_t, jnp.concatenate(hot, 1), preferred_element_type=F32)
        pad[g, lead : lead + width] = part.astype(BF16)
    fetch.wait()
    keep = classes - classes % 8
    tail[...] = jnp.zeros(tail.shape, F32)
    tail[0 : classes - keep] = table[keep:classes].astype(F32)
    last[0:8] = table[keep - 8 : keep]
    last[8:16] = tail[...].astype(BF16)
    step = width - LANES
    period = LANES // step
    tiles = period + 1
    blocks = width // period
    same = iota((blocks, GROUP, cols), 2) // leaf_num == iota((blocks, GROUP, cols), 1)
    for r in range(period):
        acc = None
        for g in range(groups):
            ref, first = (last, 0) if g == groups - 1 else (table, g * GROUP)
            rows = [ref[first : first + GROUP, (tiles * b + r) * LANES : (tiles * b + r + 2) * LANES] for b in range(blocks)]
            part = jnp.dot(jnp.concatenate(rows, 0), pad[g, lead - step * r : lead - step * r + 2 * LANES], preferred_element_type=F32)
            acc = part if acc is None else acc + part
        acc = jnp.where(same, acc.reshape(blocks, GROUP, cols), 0.0)
        acc = jnp.sum(acc, axis=1)
        for h in range(cols // LANES):
            sums[h, pl.ds(r, blocks, stride=period), :] = acc[:, h * LANES : (h + 1) * LANES]
    fold = jnp.where(iota((leaf_num, cols), 1) % leaf_num == iota((leaf_num, cols), 0), 1.0, 0.0)
    whole = jnp.concatenate([sums[h] for h in range(cols // LANES)], 1)
    expansion = lax.dot_general(fold, whole, (((1,), (1,)), ((), ())), precision=lax.Precision.HIGHEST, preferred_element_type=F32)
    fetch_down.wait()
    which = iota((leaf_num, width), 0)
    field = [None] * quads
    for leaf in range(leaf_num):
        lhs = jnp.where(which == leaf, expansion, 0.0).astype(BF16)
        for q in range(0, quads, 2):
            both = [down[leaf, i] for i in range(q, min(q + 2, quads))]
            part = jnp.dot(lhs, jnp.concatenate(both, 1), preferred_element_type=F32)
            field[q] = part if field[q] is None else field[q] + part
    quad = [field[q - q % 2][:, (q % 2) * LANES : (q % 2 + 1) * LANES] for q in range(quads)]
    for leaf in range(leaf_num):
        at = slice(leaf * LANES, (leaf + 1) * LANES)
        far = []
        for k in range(3):
            far.append(sum(own_ref[3 + c : 4 + c, at] * quad[3 * c + k][leaf : leaf + 1] for c in range(3)))
        out_ref[:, at] = near_ref[:, at] + jnp.concatenate(far, 0)


SMEM = pl.BlockSpec(memory_space=pltpu.SMEM)
VMEM = pl.BlockSpec(memory_space=pltpu.VMEM)
HBM = pl.BlockSpec(memory_space=pltpu.HBM)


def held(x, space=pltpu.VMEM):
    return pltpu.with_memory_space_constraint(x, space)


def call(body, outs, limit, **options):
    if outs is not None:
        shapes = tuple(pltpu.VMEM(o[:-1], o[-1]) for o in outs)
        options["out_shape"] = shapes if len(shapes) > 1 else shapes[0]
    params = pltpu.CompilerParams(vmem_limit_bytes=limit * 2**20)
    return pl.pallas_call(body, compiler_params=params, **options)


def per_device(positions, densities, near_src, near_count, far_slot, far_class, far_count, requests, up_basis, transfer_table, down_basis):
    leaf_num, slot_num = near_src.shape
    nodes = positions.shape[1]
    width = up_basis.shape[1]
    far_num = far_slot.shape[1]
    peers = requests.shape[1]
    classes = transfer_table.shape[0]
    groups = -(-classes // GROUP)
    rows = leaf_num * width // LANES
    up = [(i, i + 1) for i in range(peers - 1)]
    down = [(j, i) for i, j in up]
    slots = leaf_num * far_num
    own, message = call(
        front_body,
        [(8, nodes + LANES, F32), (peers * rows, LANES, BF16)],
        8,
        in_specs=[HBM] * 5,
        scratch_shapes=[
            pltpu.VMEM((3, nodes), F32),
            pltpu.VMEM((3, nodes), F32),
            pltpu.VMEM((slot_num, leaf_num), jnp.int32),
            pltpu.VMEM((1, leaf_num), jnp.int32),
            pltpu.VMEM(up_basis.shape, BF16),
            pltpu.SemaphoreType.DMA((5,)),
        ],
    )(*[held(x, pltpu.HBM) for x in (positions, densities, near_src.T, near_count[None], up_basis)])
    left = lax.ppermute(own, "patch", up)
    right = lax.ppermute(own, "patch", down)
    message = message.reshape(peers, rows // 2, 2, LANES)
    table = lax.all_to_all(message, "patch", split_axis=0, concat_axis=0, tiled=True)
    table = table.reshape(peers * rows, LANES)
    down_flat = down_basis.transpose(0, 2, 1, 3)
    near, *kept = call(
        middle_body,
        [
            (3, nodes, F32),
            (slots, peers * rows // 2, BF16),
            (slots, peers * rows // 2, BF16),
            (slots, LANES, BF16),
            (slots, LANES, BF16),
        ],
        14,
        in_specs=[VMEM] * 3 + [SMEM] + [VMEM] * 3,
        scratch_shapes=[
            pltpu.VMEM((3 * leaf_num, 8, LANES), F32),
            pltpu.VMEM((leaf_num + 1, LANES, 48), BF16),
            pltpu.VMEM((3 * leaf_num, 48, 4 * LANES), BF16),
            pltpu.VMEM((leaf_num + 1, 5, LANES, LANES), F32),
            pltpu.VMEM((LANES, 4 * LANES), F32),
            pltpu.VMEM((LANES, 4 * LANES), F32),
            pltpu.VMEM((3, slot_num, LANES), jnp.int32),
            pltpu.SMEM((3, slot_num, LANES), jnp.int32),
            pltpu.SMEM((4 * leaf_num * slot_num + 8,), jnp.int32),
            pltpu.SemaphoreType.DMA,
            pltpu.VMEM((LANES, LANES), F32),
        ],
    )(held(own), held(left), held(right), far_count, far_slot, far_class, requests[0].T)
    return call(
        far_body,
        None,
        30,
        in_specs=[VMEM] * 7 + [HBM] * 2,
        out_shape=jax.ShapeDtypeStruct((3, nodes), F32),
        scratch_shapes=[
            pltpu.VMEM(transfer_table.shape, BF16),
            pltpu.VMEM(down_flat.shape, BF16),
            pltpu.VMEM((groups, 4 * LANES - width, GROUP * leaf_num), BF16),
            pltpu.VMEM((GROUP * leaf_num // LANES, width, LANES), F32),
            pltpu.VMEM((8, width * width), F32),
            pltpu.VMEM((GROUP, width * width), BF16),
            pltpu.SemaphoreType.DMA((2,)),
        ],
    )(*[held(x) for x in (table, *kept, own, near)], held(transfer_table, pltpu.HBM), held(down_flat, pltpu.HBM))


def solution(mesh):
    placed = (
        P(None, "patch"),
        P(None, "patch"),
        P("patch", None),
        P("patch"),
        P("patch", None),
        P("patch", None),
        P("patch"),
        P("patch", None, None),
        P("patch", None, None),
        P(),
        P("patch", None, None, None),
    )
    return jax.shard_map(per_device, mesh=mesh, in_specs=placed, out_specs=P(None, "patch"), check_vma=False)
```

time: 81.7 us -> 62.8 us (0.77)
  the two profiles are of different devices: /device:TPU:24 before, /device:TPU:8 now
where the time goes in v2:
time: 62.8 us; the launch traced here: 62.6 us
  Pallas kernels  35.1 us (56%)
  starting transfers between devices  19.5 us (31%)
  waiting for transfers between devices  7.91 us (13%)
    pallas_call x1, Pallas kernels, per_device(): call(middle_body, [(3, nodes, F32), (slots, peers * rows // 2, BF16), (sl...  20.1 us
    pallas_call x1, Pallas kernels, per_device(): call(far_body, None, 30, in_specs=[VMEM] * 7 + [HBM] * 2, out_shape=jax.S...  12.1 us
    all_to_all x1, starting transfers between devices, per_device(): lax.all_to_all(message, 'patch', split_axis=0, concat_axis=0, tiled=True)  10.5 us
    ppermute x1, waiting for transfers between devices, per_device(): left = lax.ppermute(own, 'patch', up)  7.91 us
    ppermute x1, starting transfers between devices, per_device(): right = lax.ppermute(own, 'patch', down)  7.13 us
    pallas_call x1, Pallas kernels, per_device(): call(front_body, [(8, nodes + LANES, F32), (peers * rows, LANES, BF16)],...  2.96 us
    ppermute x1, starting transfers between devices, per_device(): left = lax.ppermute(own, 'patch', up)  1.92 us
  transfers between devices with their start and end apart: 3, of which 1 were waited for; matrix products, arithmetic and copies ran while one was open for 0% of the time, Pallas kernels for 32%

profile of v2, /device:TPU:8, one launch (start us, length us, event | category | flops | bytes accessed | tf_op | source)
XLA Modules:
  0.0 62.6 jit_solution(3381344142076277466)
XLA Ops:
  0.0 0.0 copy-start.2
  0.0 0.0 copy-start.3
  0.0 0.0 copy-start.1
  0.0 0.0 copy-start
  0.0 3.0 %shard_map.109 = (f32[8,2176]{1,0:T(8,128)S(1)}, bf16[2304,128]{1,0:T(8,128)(2,1)}) custom-call(f32[3,2048]{1,0:T(4,128)} %pos_hbm.1, f32[3,2048]{1,0:T(4,128)} %dens_hbm.1, s32[8,16]{1,0:T(8,128)} %bitcast.11, s32[1,16]{1,0:T(1,128)} %bitcast.12, bf16[16,144,384]{2,1,0:T(8,128)(2,1)} %up_hbm.1), custom_call_target="tpu_custom_call" | custom-call | tf_op jit(solution)/shard_map/pallas_call | solution.py:340
  3.0 10.5 %all-to-all-start = ((bf16[128,9,2,128]{3,2,1,0:T(2,128)(2,1)}), bf16[128,9,2,128]{3,2,1,0:T(2,128)(2,1)S(1)}, u32[]{:S(2)}, u32[]{:S(2)}) async-start(bf16[128,9,2,128]{3,2,1,0:T(2,128)(2,1)} %bitcast.2), calls=%async_computation | async-start | bytes 1179648 | tf_op jit(solution)/shard_map/all_to_all | solution.py:357
  13.4 7.1 %collective-permute-start.1 = (f32[8,2176]{1,0:T(8,128)S(1)}, f32[8,2176]{1,0:T(8,128)S(1)}, u32[]{:S(2)}, u32[]{:S(2)}) collective-permute-start(f32[8,2176]{1,0:T(8,128)S(1)} %get-tuple-element.13.own_ref), channel_id=1, source_target_pairs={{1,0},{2,1},{3,2},{4,3},{5,4},{6,5},{7,6},{8,7},{9,8},{10,9},{11,1... | collective-permute-start | bytes 208904 | tf_op jit(solution)/shard_map/ppermute | solution.py:355
  20.6 1.9 %collective-permute-start = (f32[8,2176]{1,0:T(8,128)S(1)}, f32[8,2176]{1,0:T(8,128)S(1)}, u32[]{:S(2)}, u32[]{:S(2)}) collective-permute-start(f32[8,2176]{1,0:T(8,128)S(1)} %get-tuple-element.13.own_ref), channel_id=1, source_target_pairs={{0,1},{1,2},{2,3},{3,4},{4,5},{5,6},{6,7},{7,8},{8,9},{9,10},{10,1... | collective-permute-start | bytes 208904 | tf_op jit(solution)/shard_map/ppermute | solution.py:354
  22.5 0.0 collective-permute-done.1.right_ref
  22.5 7.9 %collective-permute-done.left_ref = f32[8,2176]{1,0:T(8,128)S(1)} collective-permute-done((f32[8,2176]{1,0:T(8,128)S(1)}, f32[8,2176]{1,0:T(8,128)S(1)}, u32[]{:S(2)}, u32[]{:S(2)}) %collective-permute-start) | collective-permute-done | bytes 69664 | tf_op jit(solution)/shard_map/ppermute | solution.py:354
  30.4 0.0 copy-done.2
  30.4 0.0 copy-done.3
  30.4 0.0 copy-done.1
  30.4 0.0 copy-done
  30.4 20.1 %shard_map.110 = (f32[3,2048]{1,0:T(4,128)S(1)}, bf16[512,1152]{1,0:T(8,128)(2,1)S(1)}, bf16[512,1152]{1,0:T(8,128)(2,1)S(1)}, bf16[512,128]{1,0:T(8,128)(2,1)S(1)}, bf16[512,128]{1,0:T(8,128)(2,1)S(1)}) custom-call(f32[8,2176]{1,0:T(8,128)S(1)} %get-tuple-element.13.own_ref, f32[8,2176]{1,0:T(8,128)S(1)} %collective-permute-done.left_ref, ...), custom_call_target="tpu_custom_call" | custom-call | tf_op jit(solution)/shard_map/pallas_call | solution.py:360
  50.5 0.0 all-to-all-done
  50.5 12.1 %shard_map.111 = f32[3,2048]{1,0:T(4,128)} custom-call(bf16[2304,128]{1,0:T(8,128)(2,1)S(1)} %bitcast.8, bf16[512,1152]{1,0:T(8,128)(2,1)S(1)} %get-tuple-element.14.main_ref, bf16[512,1152]{1,0:T(8,128)(2,1)S(1)} %get-tuple-element.15.tail_ref, bf16[512,128]{1,0:T(8,128)(2,1)S(1)} %get-tuple-element.16.code_ref, ...), custom_call_target="tpu_custom_call" | custom-call | tf_op jit(solution)/shard_map/pallas_call | solution.py:385
Async XLA Ops:
  0.0 30.4 %copy-start.2 = (s32[1,128,4]{1,2,0:T(4,128)S(1)}, s32[1,128,4]{1,2,0:T(4,128)}, u32[]{:S(2)}) copy-start(s32[1,128,4]{1,2,0:T(4,128)} %param.18) | copy-start | bytes 6148
  0.0 30.4 %copy-start.3 = (s32[16]{0:T(128)S(1)}, s32[16]{0:T(128)}, u32[]{:S(2)}) copy-start(s32[16]{0:T(128)} %count_ref.1) | copy-start | bytes 196
  0.0 30.4 %copy-start.1 = (s32[16,32]{1,0:T(8,128)S(1)}, s32[16,32]{1,0:T(8,128)}, u32[]{:S(2)}) copy-start(s32[16,32]{1,0:T(8,128)} %class_ref.1) | copy-start | bytes 6148
  0.0 30.4 %copy-start = (s32[16,32]{1,0:T(8,128)S(1)}, s32[16,32]{1,0:T(8,128)}, u32[]{:S(2)}) copy-start(s32[16,32]{1,0:T(8,128)} %slot_ref.1) | copy-start | bytes 6148
  3.0 47.5 %all-to-all-start = ((bf16[128,9,2,128]{3,2,1,0:T(2,128)(2,1)}), bf16[128,9,2,128]{3,2,1,0:T(2,128)(2,1)S(1)}, u32[]{:S(2)}, u32[]{:S(2)}) async-start(bf16[128,9,2,128]{3,2,1,0:T(2,128)(2,1)} %bitcast.2), calls=%async_computation | async-start | bytes 1179648 | tf_op jit(solution)/shard_map/all_to_all | solution.py:357
  13.4 9.1 %collective-permute-start.1 = (f32[8,2176]{1,0:T(8,128)S(1)}, f32[8,2176]{1,0:T(8,128)S(1)}, u32[]{:S(2)}, u32[]{:S(2)}) collective-permute-start(f32[8,2176]{1,0:T(8,128)S(1)} %get-tuple-element.13.own_ref), channel_id=1, source_target_pairs={{1,0},{2,1},{3,2},{4,3},{5,4},{6,5},{7,6},{8,7},{9,8},{10,9},{11,1... | collective-permute-start | bytes 208904 | tf_op jit(solution)/shard_map/ppermute | solution.py:355
  20.6 9.8 %collective-permute-start = (f32[8,2176]{1,0:T(8,128)S(1)}, f32[8,2176]{1,0:T(8,128)S(1)}, u32[]{:S(2)}, u32[]{:S(2)}) collective-permute-start(f32[8,2176]{1,0:T(8,128)S(1)} %get-tuple-element.13.own_ref), channel_id=1, source_target_pairs={{0,1},{1,2},{2,3},{3,4},{4,5},{5,6},{6,7},{7,8},{8,9},{9,10},{10,1... | collective-permute-start | bytes 208904 | tf_op jit(solution)/shard_map/ppermute | solution.py:354

commit v3 on v2

--- a/solution.py
+++ b/solution.py
@@ -1,3 +1,4 @@
+import functools
 import math
 
 import jax
@@ -11,6 +12,8 @@
 KERNEL = 1.0 / (8.0 * math.pi)
 BLOB = 0.25
 LANES = 128
+DEPTH = 2
+EARLY = 2
 GROUP = 16
 F32 = jnp.float32
 BF16 = jnp.bfloat16
@@ -106,9 +109,28 @@
     return [jnp.concatenate(rows, 0).astype(BF16) for rows in (rho, ab, ar, br)]
 
 
-def middle_body(own_ref, left_ref, right_ref, count_ref, slot_ref, class_ref, req_ref, near_ref, main_ref, tail_ref, code_ref, kind_ref, win, lhs, rhs, acc, one, two, list_v, list_s, pairs, sem, flip):
+def middle_body(rows, own_ref, left_ref, right_ref, count_ref, slot_ref, class_ref, req_ref, table_hbm, near_ref, main_ref, tail_ref, code_ref, kind_ref, kept_ref, table, sem_table, win, lhs, rhs, acc, one, two, list_v, list_s, pairs, sem, flip):
+    fetch = pltpu.make_async_copy(table_hbm, table, sem_table)
+    fetch.start()
     near_terms(own_ref, left_ref, right_ref, near_ref, win, lhs, rhs, acc, one, two, list_v, list_s, pairs, sem)
-    select_terms(count_ref, slot_ref, class_ref, req_ref, main_ref, tail_ref, code_ref, kind_ref, flip)
+    fetch.wait()
+    keep_rows(table, kept_ref)
+    select_terms(rows, count_ref, slot_ref, class_ref, req_ref, main_ref, tail_ref, code_ref, kind_ref, flip)
+
+
+def keep_rows(table, kept_ref):
+    first = kept_ref.shape[0] - GROUP
+    classes = table.shape[0]
+    kept_ref[:first] = table[:first]
+    whole = classes - classes % 8
+    start = (classes - 1) // GROUP * GROUP
+    width = 9 * LANES
+    for at in range(0, table.shape[1], width):
+        cols = slice(at, at + width)
+        tail = table[whole:classes, cols].astype(F32)
+        tail = jnp.concatenate([tail, jnp.zeros((start + GROUP - classes, width), F32)], 0)
+        both = jnp.concatenate([table[start:whole, cols].astype(F32), tail], 0)
+        kept_ref[first:, cols] = both.astype(BF16)
 
 
 def near_terms(own_ref, left_ref, right_ref, near_ref, win, lhs, rhs, acc, one, two, list_v, list_s, pairs, sem):
@@ -116,10 +138,15 @@
     nodes = leaf_num * LANES
     slots = list_v.shape[1]
     device = lax.axis_index("patch")
-    offset = (device - 1) * leaf_num + 1
     halo = (left_ref, own_ref, right_ref)
+    leaf_of = iota((slots, LANES), 1)
     for place, ref in enumerate(halo):
-        list_v[place] = ref[:, nodes:].astype(jnp.int32)
+        listed = ref[:, nodes:].astype(jnp.int32)
+        source = listed - (device * leaf_num + 1)
+        mine = (listed > 0) & (source >= 0) & (source < leaf_num)
+        list_v[place] = jnp.where(mine, (source << 6) + (leaf_of + place * leaf_num), -1)
+        if place == 1:
+            list_v[3] = jnp.where(listed > 0, (leaf_of << 6) + (source + leaf_num), -1)
     copy = pltpu.make_async_copy(list_v, list_s, sem)
     copy.start()
     acc[...] = jnp.zeros(acc.shape, F32)
@@ -133,31 +160,26 @@
                 lhs[leaf] = target_rows(tile).T.astype(BF16)
     lhs[leaf_num] = jnp.zeros(lhs.shape[1:], BF16)
     copy.wait()
-    count = 0
-    for place in range(3):
-        def scan(leaf, count):
+
+    def scan(leaf, count):
+        for place in range(list_s.shape[0]):
             for slot in range(slots):
-                listed = list_s[place, slot, leaf]
-                source = listed - offset
-                mine = (listed > 0) & (source >= leaf_num) & (source < 2 * leaf_num)
-                pairs[count] = (source - leaf_num) * 64 + (place * leaf_num + leaf)
-                count = count + mine.astype(jnp.int32)
-                if place == 1:
-                    pairs[count] = leaf * 64 + source
-                    count = count + (listed > 0).astype(jnp.int32)
-            return count
-
-        count = lax.fori_loop(0, leaf_num, scan, count)
-    for i in range(3):
+                code = list_s[place, slot, leaf]
+                pairs[count] = code
+                count = count + (code >= 0).astype(jnp.int32)
+        return count
+
+    count = lax.fori_loop(0, leaf_num, scan, 0)
+    for i in range(3 * DEPTH):
         pairs[count + i] = leaf_num * 64
 
     def products(at, buf):
         pair = pairs[at]
-        buf[...] = jnp.dot(lhs[pair // 64], rhs[pair % 64], preferred_element_type=F32)
+        buf[...] = jnp.dot(lhs[pair >> 6], rhs[pair & 63], preferred_element_type=F32)
 
     def add_terms(at, buf):
         pair = pairs[at]
-        target, source = pair // 64, pair % 64
+        target, source = pair >> 6, pair & 63
         row = [jnp.broadcast_to(win[source, k : k + 1], (8, LANES)) for k in range(6)]
         for part in range(LANES // 8):
             i = slice(part * 8, part * 8 + 8)
@@ -172,16 +194,22 @@
             for k in range(3):
                 acc[target, 2 + k, i] += row[3 + k] * ar + row[k] * coef
 
-    products(0, one)
-
-    def two_blocks(step, _):
-        products(2 * step + 1, two)
-        add_terms(2 * step, one)
-        products(2 * step + 2, one)
-        add_terms(2 * step + 1, two)
+    for i in range(DEPTH):
+        products(i, one.at[i])
+
+    def blocks(step, _):
+        first = step * (2 * DEPTH)
+        for i in range(DEPTH):
+            products(first + DEPTH + i, two.at[i])
+        for i in range(DEPTH):
+            add_terms(first + i, one.at[i])
+        for i in range(DEPTH):
+            products(first + 2 * DEPTH + i, one.at[i])
+        for i in range(DEPTH):
+            add_terms(first + DEPTH + i, two.at[i])
         return 0
 
-    lax.fori_loop(0, (count + 1) // 2, two_blocks, 0)
+    lax.fori_loop(0, (count + 2 * DEPTH - 1) // (2 * DEPTH), blocks, 0)
     lane = iota((LANES, LANES), 1)
     for leaf in range(leaf_num):
         flat = jnp.zeros((LANES, LANES), F32)
@@ -199,12 +227,11 @@
     return scratch[...].T
 
 
-def select_terms(count_ref, slot_ref, class_ref, req_ref, main_ref, tail_ref, code_ref, kind_ref, scratch):
+def select_terms(rows, count_ref, slot_ref, class_ref, req_ref, main_ref, tail_ref, code_ref, kind_ref, scratch):
     leaf_num, far_num = slot_ref.shape
     cap, peers = req_ref.shape
     reps = LANES // leaf_num
     half = peers // 2
-    rows = main_ref.shape[1] // half
     scratch[...] = jnp.zeros((LANES, LANES), F32)
     asked = columns(scratch, req_ref[...])
     asked = jnp.concatenate([jnp.broadcast_to(asked[:, t : t + 1], (peers, LANES)) for t in range(cap)], 0)
@@ -214,9 +241,8 @@
     lane = iota((far_num, LANES), 1)
     row = iota((far_num, LANES), 0)
 
-    def hots(ref, at, key, stride):
-        for t in range(ref.shape[1] // LANES):
-            ref[at, t * LANES : (t + 1) * LANES] = jnp.where(key == t * stride, 1.0, 0.0).astype(BF16)
+    def code(row):
+        return jnp.where(lane == row % LANES, row // LANES, -1).astype(BF16)
 
     for leaf in range(leaf_num):
         at = slice(leaf * far_num, (leaf + 1) * far_num)
@@ -226,27 +252,34 @@
         picks = [jnp.where(key == t * peers, 1.0, 0.0).astype(BF16) for t in range(cap)]
         local = jnp.dot(jnp.concatenate(picks, 1), asked, preferred_element_type=F32).astype(jnp.int32)
         upper = (peer >= half).astype(jnp.int32)
-        base = (peer - upper * half) * rows - lane
-        hots(main_ref, at, base + local, LANES)
-        hots(tail_ref, at, base + leaf_num + local // reps, LANES)
+        base = (peer - upper * half) * rows
+        main_ref[at] = code(base + local)
+        tail_ref[at] = code(base + leaf_num + local // reps)
         code_ref[at] = (upper + 2 * (lane // leaf_num == local % reps).astype(jnp.int32)).astype(BF16)
         kind = jnp.broadcast_to(classes[:far_num, leaf : leaf + 1], (far_num, LANES)).astype(jnp.int32)
         keep = (lane % leaf_num == leaf) & (row < count_ref[leaf])
         kind_ref[at] = jnp.where(keep, kind - lane // leaf_num, -LANES).astype(BF16)
 
 
-def far_body(mom_ref, main_ref, tail_ref, code_ref, kind_ref, own_ref, near_ref, table_hbm, down_hbm, out_ref, table, down, pad, sums, tail, last, sem):
-    fetch = pltpu.make_async_copy(table_hbm, table, sem.at[0])
+def far_body(mom_ref, main_ref, tail_ref, code_ref, kind_ref, kept_ref, own_ref, near_ref, table_hbm, down_hbm, out_ref, table, down, pad, sums, sem):
+    early = kept_ref.shape[0] - GROUP
+    fetch = pltpu.make_async_copy(table_hbm.at[pl.ds(early, table.shape[0])], table, sem.at[0])
     fetch_down = pltpu.make_async_copy(down_hbm, down, sem.at[1])
     fetch.start()
     fetch_down.start()
     leaf_num, quads, width, _ = down.shape
-    classes = table.shape[0]
     groups = pad.shape[0]
     half = mom_ref.shape[0] // 2
     both = jnp.concatenate([mom_ref[:half], mom_ref[half:]], 1)
-    main = jnp.dot(main_ref[...], both, preferred_element_type=F32)
-    tails = jnp.dot(tail_ref[...], both, preferred_element_type=F32)
+    one, zero = jnp.ones((), BF16), jnp.zeros((), BF16)
+
+    def hots(ref, count, stride=1):
+        codes = ref[...]
+        return [jnp.where(codes == i * stride, one, zero) for i in range(count)]
+
+    tiles = half // LANES
+    main = jnp.dot(jnp.concatenate(hots(main_ref, tiles), 1), both, preferred_element_type=F32)
+    tails = jnp.dot(jnp.concatenate(hots(tail_ref, tiles), 1), both, preferred_element_type=F32)
     code = code_ref[...].astype(F32)
     upper = (code == 1.0) | (code == 3.0)
     main = jnp.where(upper, main[:, LANES:], main[:, :LANES]).T
@@ -255,22 +288,16 @@
     extra = width - LANES
     tails = sum(tails[i * extra : (i + 1) * extra] for i in range(LANES // extra))
     src_t = jnp.concatenate([main, tails], 0).astype(BF16)
-    kind = kind_ref[...]
-    one, zero = jnp.ones((), BF16), jnp.zeros((), BF16)
     lead = 2 * LANES - width
     cols = GROUP * leaf_num
+    per = cols // LANES
+    hot = hots(kind_ref, groups * per, LANES // leaf_num)
     for g in range(groups):
         pad[g, 0:lead] = jnp.zeros((lead, cols), BF16)
         pad[g, lead + width :] = jnp.zeros((pad.shape[1] - lead - width, cols), BF16)
-        hot = [jnp.where(kind == (g * (cols // LANES) + h) * (LANES // leaf_num), one, zero) for h in range(cols // LANES)]
-        part = jnp.dot(src_t, jnp.concatenate(hot, 1), preferred_element_type=F32)
+        part = jnp.dot(src_t, jnp.concatenate(hot[g * per : (g + 1) * per], 1), preferred_element_type=F32)
         pad[g, lead : lead + width] = part.astype(BF16)
     fetch.wait()
-    keep = classes - classes % 8
-    tail[...] = jnp.zeros(tail.shape, F32)
-    tail[0 : classes - keep] = table[keep:classes].astype(F32)
-    last[0:8] = table[keep - 8 : keep]
-    last[8:16] = tail[...].astype(BF16)
     step = width - LANES
     period = LANES // step
     tiles = period + 1
@@ -279,7 +306,12 @@
     for r in range(period):
         acc = None
         for g in range(groups):
-            ref, first = (last, 0) if g == groups - 1 else (table, g * GROUP)
+            if g == groups - 1:
+                ref, first = kept_ref, early
+            elif g * GROUP < early:
+                ref, first = kept_ref, g * GROUP
+            else:
+                ref, first = table, g * GROUP - early
             rows = [ref[first : first + GROUP, (tiles * b + r) * LANES : (tiles * b + r + 2) * LANES] for b in range(blocks)]
             part = jnp.dot(jnp.concatenate(rows, 0), pad[g, lead - step * r : lead - step * r + 2 * LANES], preferred_element_type=F32)
             acc = part if acc is None else acc + part
@@ -358,43 +390,44 @@
     table = table.reshape(peers * rows, LANES)
     down_flat = down_basis.transpose(0, 2, 1, 3)
     near, *kept = call(
-        middle_body,
+        functools.partial(middle_body, rows),
         [
             (3, nodes, F32),
-            (slots, peers * rows // 2, BF16),
-            (slots, peers * rows // 2, BF16),
             (slots, LANES, BF16),
             (slots, LANES, BF16),
+            (slots, LANES, BF16),
+            (slots, LANES, BF16),
+            ((EARLY + 1) * GROUP, width * width, BF16),
         ],
-        14,
-        in_specs=[VMEM] * 3 + [SMEM] + [VMEM] * 3,
+        36,
+        in_specs=[VMEM] * 3 + [SMEM] + [VMEM] * 3 + [HBM],
         scratch_shapes=[
+            pltpu.VMEM(transfer_table.shape, BF16),
+            pltpu.SemaphoreType.DMA,
             pltpu.VMEM((3 * leaf_num, 8, LANES), F32),
             pltpu.VMEM((leaf_num + 1, LANES, 48), BF16),
             pltpu.VMEM((3 * leaf_num, 48, 4 * LANES), BF16),
             pltpu.VMEM((leaf_num + 1, 5, LANES, LANES), F32),
-            pltpu.VMEM((LANES, 4 * LANES), F32),
-            pltpu.VMEM((LANES, 4 * LANES), F32),
-            pltpu.VMEM((3, slot_num, LANES), jnp.int32),
-            pltpu.SMEM((3, slot_num, LANES), jnp.int32),
-            pltpu.SMEM((4 * leaf_num * slot_num + 8,), jnp.int32),
+            pltpu.VMEM((DEPTH, LANES, 4 * LANES), F32),
+            pltpu.VMEM((DEPTH, LANES, 4 * LANES), F32),
+            pltpu.VMEM((4, slot_num, LANES), jnp.int32),
+            pltpu.SMEM((4, slot_num, LANES), jnp.int32),
+            pltpu.SMEM((4 * leaf_num * slot_num + 3 * DEPTH,), jnp.int32),
             pltpu.SemaphoreType.DMA,
             pltpu.VMEM((LANES, LANES), F32),
         ],
-    )(held(own), held(left), held(right), far_count, far_slot, far_class, requests[0].T)
+    )(held(own), held(left), held(right), far_count, far_slot, far_class, requests[0].T, held(transfer_table, pltpu.HBM))
     return call(
         far_body,
         None,
         30,
-        in_specs=[VMEM] * 7 + [HBM] * 2,
+        in_specs=[VMEM] * 8 + [HBM] * 2,
         out_shape=jax.ShapeDtypeStruct((3, nodes), F32),
         scratch_shapes=[
-            pltpu.VMEM(transfer_table.shape, BF16),
+            pltpu.VMEM(((groups - 1 - EARLY) * GROUP, width * width), BF16),
             pltpu.VMEM(down_flat.shape, BF16),
             pltpu.VMEM((groups, 4 * LANES - width, GROUP * leaf_num), BF16),
             pltpu.VMEM((GROUP * leaf_num // LANES, width, LANES), F32),
-            pltpu.VMEM((8, width * width), F32),
-            pltpu.VMEM((GROUP, width * width), BF16),
             pltpu.SemaphoreType.DMA((2,)),
         ],
     )(*[held(x) for x in (table, *kept, own, near)], held(transfer_table, pltpu.HBM), held(down_flat, pltpu.HBM))

time: 62.8 us -> 60.9 us (0.970)
  Pallas kernels: 35.1 us -> 30.3 us
  local copies, waits for them, and re-layouts: 0.02 us -> 2.73 us
    pallas_call x2, Pallas kernels: 32.1 us -> 27.4 us  [the longest x1 16 us: per_device(): call(functools.partial(middle_body, rows), [(3, nodes, F32), (slots, LANE...]
    unnamed x8, local copies, waits for them, and re-layouts: 0.02 us -> 2.73 us
  transfers between devices with their start and end apart: 3 -> 3, of which waited for: 1 -> 1; matrix products, arithmetic and copies ran while one was open for 0% -> 0% of each run, Pallas kernels for 32% -> 27%
where the time goes in v3:
time: 60.9 us; the launch traced here: 60.5 us
  Pallas kernels  30.3 us (50%)
  starting transfers between devices  19.5 us (32%)
  waiting for transfers between devices  7.91 us (13%)
  local copies, waits for them, and re-layouts  2.73 us (4%)
    pallas_call x1, Pallas kernels, per_device(): call(functools.partial(middle_body, rows), [(3, nodes, F32), (slots, LANE...  16 us
    pallas_call x1, Pallas kernels, per_device(): call(far_body, None, 30, in_specs=[VMEM] * 8 + [HBM] * 2, out_shape=jax.S...  11.4 us
    all_to_all x1, starting transfers between devices, per_device(): lax.all_to_all(message, 'patch', split_axis=0, concat_axis=0, tiled=True)  10.5 us
    ppermute x1, waiting for transfers between devices, per_device(): left = lax.ppermute(own, 'patch', up)  7.91 us
    ppermute x1, starting transfers between devices, per_device(): right = lax.ppermute(own, 'patch', down)  7.13 us
    pallas_call x1, Pallas kernels, per_device(): call(front_body, [(8, nodes + LANES, F32), (peers * rows, LANES, BF16)],...  2.91 us
    unnamed x8, local copies, waits for them, and re-layouts  2.73 us
    ppermute x1, starting transfers between devices, per_device(): left = lax.ppermute(own, 'patch', up)  1.92 us
  transfers between devices with their start and end apart: 3, of which 1 were waited for; matrix products, arithmetic and copies ran while one was open for 0% of the time, Pallas kernels for 27%

profile of v3, /device:TPU:8, one launch (start us, length us, event | category | flops | bytes accessed | tf_op | source)
XLA Modules:
  0.0 60.5 jit_solution(8213061696365272484)
XLA Ops:
  0.0 2.9 %shard_map.109 = (f32[8,2176]{1,0:T(8,128)S(1)}, bf16[2304,128]{1,0:T(8,128)(2,1)}) custom-call(f32[3,2048]{1,0:T(4,128)} %pos_hbm.1, f32[3,2048]{1,0:T(4,128)} %dens_hbm.1, s32[8,16]{1,0:T(8,128)} %bitcast.11, s32[1,16]{1,0:T(1,128)} %bitcast.12, bf16[16,144,384]{2,1,0:T(8,128)(2,1)} %up_hbm.1), custom_call_target="tpu_custom_call" | custom-call | tf_op jit(solution)/shard_map/pallas_call | solution.py:372
  2.9 10.5 %all-to-all-start = ((bf16[128,9,2,128]{3,2,1,0:T(2,128)(2,1)}), bf16[128,9,2,128]{3,2,1,0:T(2,128)(2,1)S(1)}, u32[]{:S(2)}, u32[]{:S(2)}) async-start(bf16[128,9,2,128]{3,2,1,0:T(2,128)(2,1)} %bitcast.2), calls=%async_computation | async-start | bytes 1179648 | tf_op jit(solution)/shard_map/all_to_all | solution.py:389
  13.4 7.1 %collective-permute-start.1 = (f32[8,2176]{1,0:T(8,128)S(1)}, f32[8,2176]{1,0:T(8,128)S(1)}, u32[]{:S(2)}, u32[]{:S(2)}) collective-permute-start(f32[8,2176]{1,0:T(8,128)S(1)} %get-tuple-element.14.own_ref), channel_id=1, source_target_pairs={{1,0},{2,1},{3,2},{4,3},{5,4},{6,5},{7,6},{8,7},{9,8},{10,9},{11,1... | collective-permute-start | bytes 208904 | tf_op jit(solution)/shard_map/ppermute | solution.py:387
  20.5 1.9 %collective-permute-start = (f32[8,2176]{1,0:T(8,128)S(1)}, f32[8,2176]{1,0:T(8,128)S(1)}, u32[]{:S(2)}, u32[]{:S(2)}) collective-permute-start(f32[8,2176]{1,0:T(8,128)S(1)} %get-tuple-element.14.own_ref), channel_id=1, source_target_pairs={{0,1},{1,2},{2,3},{3,4},{4,5},{5,6},{6,7},{7,8},{8,9},{9,10},{10,1... | collective-permute-start | bytes 208904 | tf_op jit(solution)/shard_map/ppermute | solution.py:386
  22.4 0.0 collective-permute-done.1.right_ref
  22.5 7.9 %collective-permute-done.left_ref = f32[8,2176]{1,0:T(8,128)S(1)} collective-permute-done((f32[8,2176]{1,0:T(8,128)S(1)}, f32[8,2176]{1,0:T(8,128)S(1)}, u32[]{:S(2)}, u32[]{:S(2)}) %collective-permute-start) | collective-permute-done | bytes 69664 | tf_op jit(solution)/shard_map/ppermute | solution.py:386
  30.4 0.0 copy-start
  30.4 0.7 %copy-done = s32[16,32]{1,0:T(8,128)S(1)} copy-done((s32[16,32]{1,0:T(8,128)S(1)}, s32[16,32]{1,0:T(8,128)}, u32[]{:S(2)}) %copy-start) | copy-done | bytes 2072
  31.1 0.0 copy-start.1
  31.1 0.7 %copy-done.1 = s32[16,32]{1,0:T(8,128)S(1)} copy-done((s32[16,32]{1,0:T(8,128)S(1)}, s32[16,32]{1,0:T(8,128)}, u32[]{:S(2)}) %copy-start.1) | copy-done | bytes 2072
  31.8 0.0 copy-start.2
  31.8 0.7 %copy-done.2 = s32[1,128,4]{1,2,0:T(4,128)S(1)} copy-done((s32[1,128,4]{1,2,0:T(4,128)S(1)}, s32[1,128,4]{1,2,0:T(4,128)}, u32[]{:S(2)}) %copy-start.2) | copy-done | bytes 2072
  32.4 0.0 copy-start.3
  32.4 0.7 %copy-done.3 = s32[16]{0:T(128)S(1)} copy-done((s32[16]{0:T(128)S(1)}, s32[16]{0:T(128)}, u32[]{:S(2)}) %copy-start.3) | copy-done | bytes 88
  33.1 16.0 %shard_map.110 = (f32[3,2048]{1,0:T(4,128)S(1)}, bf16[512,128]{1,0:T(8,128)(2,1)S(1)}, bf16[512,128]{1,0:T(8,128)(2,1)S(1)}, bf16[512,128]{1,0:T(8,128)(2,1)S(1)...) custom-call(f32[8,2176]{1,0:T(8,128)S(1)} %get-tuple-element.14.own_ref, ...), custom_call_target="tpu_custom_call" | custom-call | tf_op jit(solution)/shard_map/pallas_call | solution.py:392
  49.2 0.0 all-to-all-done
  49.2 11.4 %shard_map.111 = f32[3,2048]{1,0:T(4,128)} custom-call(bf16[2304,128]{1,0:T(8,128)(2,1)S(1)} %bitcast.8, bf16[512,128]{1,0:T(8,128)(2,1)S(1)} %get-tuple-element.15.main_ref, bf16[512,128]{1,0:T(8,128)(2,1)S(1)} %get-tuple-element.16.tail_ref, bf16[512,128]{1,0:T(8,128)(2,1)S(1)} %get-tuple-element.17.code_ref, ...), custom_call_target="tpu_custom_call" | custom-call | tf_op jit(solution)/shard_map/pallas_call | solution.py:420
Async XLA Ops:
  2.9 46.2 %all-to-all-start = ((bf16[128,9,2,128]{3,2,1,0:T(2,128)(2,1)}), bf16[128,9,2,128]{3,2,1,0:T(2,128)(2,1)S(1)}, u32[]{:S(2)}, u32[]{:S(2)}) async-start(bf16[128,9,2,128]{3,2,1,0:T(2,128)(2,1)} %bitcast.2), calls=%async_computation | async-start | bytes 1179648 | tf_op jit(solution)/shard_map/all_to_all | solution.py:389
  13.4 9.1 %collective-permute-start.1 = (f32[8,2176]{1,0:T(8,128)S(1)}, f32[8,2176]{1,0:T(8,128)S(1)}, u32[]{:S(2)}, u32[]{:S(2)}) collective-permute-start(f32[8,2176]{1,0:T(8,128)S(1)} %get-tuple-element.14.own_ref), channel_id=1, source_target_pairs={{1,0},{2,1},{3,2},{4,3},{5,4},{6,5},{7,6},{8,7},{9,8},{10,9},{11,1... | collective-permute-start | bytes 208904 | tf_op jit(solution)/shard_map/ppermute | solution.py:387
  20.5 9.8 %collective-permute-start = (f32[8,2176]{1,0:T(8,128)S(1)}, f32[8,2176]{1,0:T(8,128)S(1)}, u32[]{:S(2)}, u32[]{:S(2)}) collective-permute-start(f32[8,2176]{1,0:T(8,128)S(1)} %get-tuple-element.14.own_ref), channel_id=1, source_target_pairs={{0,1},{1,2},{2,3},{3,4},{4,5},{5,6},{6,7},{7,8},{8,9},{9,10},{10,1... | collective-permute-start | bytes 208904 | tf_op jit(solution)/shard_map/ppermute | solution.py:386
  30.4 0.7 %copy-start = (s32[16,32]{1,0:T(8,128)S(1)}, s32[16,32]{1,0:T(8,128)}, u32[]{:S(2)}) copy-start(s32[16,32]{1,0:T(8,128)} %slot_ref.1) | copy-start | bytes 6148
  31.1 0.7 %copy-start.1 = (s32[16,32]{1,0:T(8,128)S(1)}, s32[16,32]{1,0:T(8,128)}, u32[]{:S(2)}) copy-start(s32[16,32]{1,0:T(8,128)} %class_ref.1) | copy-start | bytes 6148
  31.8 0.7 %copy-start.2 = (s32[1,128,4]{1,2,0:T(4,128)S(1)}, s32[1,128,4]{1,2,0:T(4,128)}, u32[]{:S(2)}) copy-start(s32[1,128,4]{1,2,0:T(4,128)} %param.18) | copy-start | bytes 6148
  32.4 0.7 %copy-start.3 = (s32[16]{0:T(128)S(1)}, s32[16]{0:T(128)}, u32[]{:S(2)}) copy-start(s32[16]{0:T(128)} %count_ref.1) | copy-start | bytes 196

commit v4 on v3

--- a/solution.py
+++ b/solution.py
@@ -109,11 +109,14 @@
     return [jnp.concatenate(rows, 0).astype(BF16) for rows in (rho, ab, ar, br)]
 
 
-def middle_body(rows, own_ref, left_ref, right_ref, count_ref, slot_ref, class_ref, req_ref, table_hbm, near_ref, main_ref, tail_ref, code_ref, kind_ref, kept_ref, table, sem_table, win, lhs, rhs, acc, one, two, list_v, list_s, pairs, sem, flip):
-    fetch = pltpu.make_async_copy(table_hbm, table, sem_table)
-    fetch.start()
+def middle_body(rows, own_ref, left_ref, right_ref, count_hbm, slot_hbm, class_hbm, req_hbm, table_hbm, near_ref, main_ref, tail_ref, code_ref, kind_ref, kept_ref, table, count_ref, slot_ref, class_ref, req_ref, sems, win, lhs, rhs, acc, one, two, list_v, list_s, pairs, sem, flip):
+    pairs_of = ((table_hbm, table), (count_hbm, count_ref), (slot_hbm, slot_ref), (class_hbm, class_ref), (req_hbm, req_ref))
+    fetches = [pltpu.make_async_copy(a, b, sems.at[i]) for i, (a, b) in enumerate(pairs_of)]
+    for fetch in fetches:
+        fetch.start()
     near_terms(own_ref, left_ref, right_ref, near_ref, win, lhs, rhs, acc, one, two, list_v, list_s, pairs, sem)
-    fetch.wait()
+    for fetch in fetches:
+        fetch.wait()
     keep_rows(table, kept_ref)
     select_terms(rows, count_ref, slot_ref, class_ref, req_ref, main_ref, tail_ref, code_ref, kind_ref, flip)
 
@@ -269,34 +272,41 @@
     fetch_down.start()
     leaf_num, quads, width, _ = down.shape
     groups = pad.shape[0]
-    half = mom_ref.shape[0] // 2
-    both = jnp.concatenate([mom_ref[:half], mom_ref[half:]], 1)
-    one, zero = jnp.ones((), BF16), jnp.zeros((), BF16)
-
-    def hots(ref, count, stride=1):
-        codes = ref[...]
-        return [jnp.where(codes == i * stride, one, zero) for i in range(count)]
-
-    tiles = half // LANES
-    main = jnp.dot(jnp.concatenate(hots(main_ref, tiles), 1), both, preferred_element_type=F32)
-    tails = jnp.dot(jnp.concatenate(hots(tail_ref, tiles), 1), both, preferred_element_type=F32)
-    code = code_ref[...].astype(F32)
-    upper = (code == 1.0) | (code == 3.0)
-    main = jnp.where(upper, main[:, LANES:], main[:, :LANES]).T
-    tails = jnp.where(upper, tails[:, LANES:], tails[:, :LANES])
-    tails = jnp.where(code >= 2, tails, 0.0).T
-    extra = width - LANES
-    tails = sum(tails[i * extra : (i + 1) * extra] for i in range(LANES // extra))
-    src_t = jnp.concatenate([main, tails], 0).astype(BF16)
     lead = 2 * LANES - width
     cols = GROUP * leaf_num
-    per = cols // LANES
-    hot = hots(kind_ref, groups * per, LANES // leaf_num)
-    for g in range(groups):
-        pad[g, 0:lead] = jnp.zeros((lead, cols), BF16)
-        pad[g, lead + width :] = jnp.zeros((pad.shape[1] - lead - width, cols), BF16)
-        part = jnp.dot(src_t, jnp.concatenate(hot[g * per : (g + 1) * per], 1), preferred_element_type=F32)
-        pad[g, lead : lead + width] = part.astype(BF16)
+
+    @pl.when(lax.axis_index("patch") >= 0)
+    def _():
+        groups = pad.shape[0]
+        half = mom_ref.shape[0] // 2
+        both = jnp.concatenate([mom_ref[:half], mom_ref[half:]], 1)
+        one, zero = jnp.ones((), BF16), jnp.zeros((), BF16)
+
+        def hots(ref, count, stride=1):
+            codes = ref[...]
+            return [jnp.where(codes == i * stride, one, zero) for i in range(count)]
+
+        tiles = half // LANES
+        main = jnp.dot(jnp.concatenate(hots(main_ref, tiles), 1), both, preferred_element_type=F32)
+        tails = jnp.dot(jnp.concatenate(hots(tail_ref, tiles), 1), both, preferred_element_type=F32)
+        code = code_ref[...].astype(F32)
+        upper = (code == 1.0) | (code == 3.0)
+        main = jnp.where(upper, main[:, LANES:], main[:, :LANES]).T
+        tails = jnp.where(upper, tails[:, LANES:], tails[:, :LANES])
+        tails = jnp.where(code >= 2, tails, 0.0).T
+        extra = width - LANES
+        tails = sum(tails[i * extra : (i + 1) * extra] for i in range(LANES // extra))
+        src_t = jnp.concatenate([main, tails], 0).astype(BF16)
+        lead = 2 * LANES - width
+        cols = GROUP * leaf_num
+        per = cols // LANES
+        hot = hots(kind_ref, groups * per, LANES // leaf_num)
+        for g in range(groups):
+            pad[g, 0:lead] = jnp.zeros((lead, cols), BF16)
+            pad[g, lead + width :] = jnp.zeros((pad.shape[1] - lead - width, cols), BF16)
+            part = jnp.dot(src_t, jnp.concatenate(hot[g * per : (g + 1) * per], 1), preferred_element_type=F32)
+            pad[g, lead : lead + width] = part.astype(BF16)
+
     fetch.wait()
     step = width - LANES
     period = LANES // step
@@ -400,10 +410,14 @@
             ((EARLY + 1) * GROUP, width * width, BF16),
         ],
         36,
-        in_specs=[VMEM] * 3 + [SMEM] + [VMEM] * 3 + [HBM],
+        in_specs=[VMEM] * 3 + [HBM] * 5,
         scratch_shapes=[
             pltpu.VMEM(transfer_table.shape, BF16),
-            pltpu.SemaphoreType.DMA,
+            pltpu.SMEM(far_count.shape, jnp.int32),
+            pltpu.VMEM(far_slot.shape, jnp.int32),
+            pltpu.VMEM(far_class.shape, jnp.int32),
+            pltpu.VMEM((requests.shape[2], peers), jnp.int32),
+            pltpu.SemaphoreType.DMA((5,)),
             pltpu.VMEM((3 * leaf_num, 8, LANES), F32),
             pltpu.VMEM((leaf_num + 1, LANES, 48), BF16),
             pltpu.VMEM((3 * leaf_num, 48, 4 * LANES), BF16),
@@ -416,7 +430,7 @@
             pltpu.SemaphoreType.DMA,
             pltpu.VMEM((LANES, LANES), F32),
         ],
-    )(held(own), held(left), held(right), far_count, far_slot, far_class, requests[0].T, held(transfer_table, pltpu.HBM))
+    )(held(own), held(left), held(right), *[held(x, pltpu.HBM) for x in (far_count, far_slot, far_class, requests[0].T, transfer_table)])
     return call(
         far_body,
         None,

time: 60.9 us -> 55.9 us (0.918)
  local copies, waits for them, and re-layouts: 2.73 us -> 0 us
  Pallas kernels: 30.3 us -> 28.2 us
    unnamed x8 -> x0, local copies, waits for them, and re-layouts: 2.73 us -> none
    pallas_call x1, Pallas kernels: 11.4 us -> 9.78 us  [per_device(): call(far_body, None, 30, in_specs=[VMEM] * 8 + [HBM] * 2, out_shape=jax.S...]
  transfers between devices with their start and end apart: 3 -> 3, of which waited for: 1 -> 1; matrix products, arithmetic and copies ran while one was open for 0% -> 0% of each run, Pallas kernels for 27% -> 28%
where the time goes in v4:
time: 55.9 us; the launch traced here: 55.7 us
  Pallas kernels  28.2 us (50%)
  starting transfers between devices  19.5 us (35%)
  waiting for transfers between devices  7.91 us (14%)
    pallas_call x1, Pallas kernels, per_device(): call(functools.partial(middle_body, rows), [(3, nodes, F32), (slots, LANE...  15.5 us
    all_to_all x1, starting transfers between devices, per_device(): lax.all_to_all(message, 'patch', split_axis=0, concat_axis=0, tiled=True)  10.5 us
    pallas_call x1, Pallas kernels, per_device(): call(far_body, None, 30, in_specs=[VMEM] * 8 + [HBM] * 2, out_shape=jax.S...  9.78 us
    ppermute x1, waiting for transfers between devices, per_device(): left = lax.ppermute(own, 'patch', up)  7.91 us
    ppermute x1, starting transfers between devices, per_device(): right = lax.ppermute(own, 'patch', down)  7.13 us
    pallas_call x1, Pallas kernels, per_device(): call(front_body, [(8, nodes + LANES, F32), (peers * rows, LANES, BF16)],...  2.92 us
    ppermute x1, starting transfers between devices, per_device(): left = lax.ppermute(own, 'patch', up)  1.92 us
  transfers between devices with their start and end apart: 3, of which 1 were waited for; matrix products, arithmetic and copies ran while one was open for 0% of the time, Pallas kernels for 28%

profile of v4, /device:TPU:8, one launch (start us, length us, event | category | flops | bytes accessed | tf_op | source)
XLA Modules:
  0.0 55.7 jit_solution(9068026231213333640)
XLA Ops:
  0.0 2.9 %shard_map.109 = (f32[8,2176]{1,0:T(8,128)S(1)}, bf16[2304,128]{1,0:T(8,128)(2,1)}) custom-call(f32[3,2048]{1,0:T(4,128)} %pos_hbm.1, f32[3,2048]{1,0:T(4,128)} %dens_hbm.1, s32[8,16]{1,0:T(8,128)} %bitcast.10, s32[1,16]{1,0:T(1,128)} %bitcast.12, bf16[16,144,384]{2,1,0:T(8,128)(2,1)} %up_hbm.1), custom_call_target="tpu_custom_call" | custom-call | tf_op jit(solution)/shard_map/pallas_call | solution.py:382
  2.9 10.5 %all-to-all-start = ((bf16[128,9,2,128]{3,2,1,0:T(2,128)(2,1)}), bf16[128,9,2,128]{3,2,1,0:T(2,128)(2,1)S(1)}, u32[]{:S(2)}, u32[]{:S(2)}) async-start(bf16[128,9,2,128]{3,2,1,0:T(2,128)(2,1)} %bitcast.2), calls=%async_computation | async-start | bytes 1179648 | tf_op jit(solution)/shard_map/all_to_all | solution.py:399
  13.4 7.1 %collective-permute-start.1 = (f32[8,2176]{1,0:T(8,128)S(1)}, f32[8,2176]{1,0:T(8,128)S(1)}, u32[]{:S(2)}, u32[]{:S(2)}) collective-permute-start(f32[8,2176]{1,0:T(8,128)S(1)} %get-tuple-element.14.own_ref), channel_id=1, source_target_pairs={{1,0},{2,1},{3,2},{4,3},{5,4},{6,5},{7,6},{8,7},{9,8},{10,9},{11,1... | collective-permute-start | bytes 208904 | tf_op jit(solution)/shard_map/ppermute | solution.py:397
  20.5 1.9 %collective-permute-start = (f32[8,2176]{1,0:T(8,128)S(1)}, f32[8,2176]{1,0:T(8,128)S(1)}, u32[]{:S(2)}, u32[]{:S(2)}) collective-permute-start(f32[8,2176]{1,0:T(8,128)S(1)} %get-tuple-element.14.own_ref), channel_id=1, source_target_pairs={{0,1},{1,2},{2,3},{3,4},{4,5},{5,6},{6,7},{7,8},{8,9},{9,10},{10,1... | collective-permute-start | bytes 208904 | tf_op jit(solution)/shard_map/ppermute | solution.py:396
  22.5 0.0 collective-permute-done.1.right_ref
  22.5 7.9 %collective-permute-done.left_ref = f32[8,2176]{1,0:T(8,128)S(1)} collective-permute-done((f32[8,2176]{1,0:T(8,128)S(1)}, f32[8,2176]{1,0:T(8,128)S(1)}, u32[]{:S(2)}, u32[]{:S(2)}) %collective-permute-start) | collective-permute-done | bytes 69664 | tf_op jit(solution)/shard_map/ppermute | solution.py:396
  30.4 15.5 %shard_map.110 = (f32[3,2048]{1,0:T(4,128)S(1)}, bf16[512,128]{1,0:T(8,128)(2,1)S(1)}, bf16[512,128]{1,0:T(8,128)(2,1)S(1)}, bf16[512,128]{1,0:T(8,128)(2,1)S(1)...) custom-call(f32[8,2176]{1,0:T(8,128)S(1)} %get-tuple-element.14.own_ref, ...), custom_call_target="tpu_custom_call" | custom-call | tf_op jit(solution)/shard_map/pallas_call | solution.py:402
  45.9 0.0 all-to-all-done
  45.9 9.8 %shard_map.111 = f32[3,2048]{1,0:T(4,128)} custom-call(bf16[2304,128]{1,0:T(8,128)(2,1)S(1)} %bitcast.8, bf16[512,128]{1,0:T(8,128)(2,1)S(1)} %get-tuple-element.15.main_ref, bf16[512,128]{1,0:T(8,128)(2,1)S(1)} %get-tuple-element.16.tail_ref, bf16[512,128]{1,0:T(8,128)(2,1)S(1)} %get-tuple-element.17.code_ref, ...), custom_call_target="tpu_custom_call" | custom-call | tf_op jit(solution)/shard_map/pallas_call | solution.py:434
Async XLA Ops:
  2.9 43.0 %all-to-all-start = ((bf16[128,9,2,128]{3,2,1,0:T(2,128)(2,1)}), bf16[128,9,2,128]{3,2,1,0:T(2,128)(2,1)S(1)}, u32[]{:S(2)}, u32[]{:S(2)}) async-start(bf16[128,9,2,128]{3,2,1,0:T(2,128)(2,1)} %bitcast.2), calls=%async_computation | async-start | bytes 1179648 | tf_op jit(solution)/shard_map/all_to_all | solution.py:399
  13.4 9.1 %collective-permute-start.1 = (f32[8,2176]{1,0:T(8,128)S(1)}, f32[8,2176]{1,0:T(8,128)S(1)}, u32[]{:S(2)}, u32[]{:S(2)}) collective-permute-start(f32[8,2176]{1,0:T(8,128)S(1)} %get-tuple-element.14.own_ref), channel_id=1, source_target_pairs={{1,0},{2,1},{3,2},{4,3},{5,4},{6,5},{7,6},{8,7},{9,8},{10,9},{11,1... | collective-permute-start | bytes 208904 | tf_op jit(solution)/shard_map/ppermute | solution.py:397
  20.5 9.8 %collective-permute-start = (f32[8,2176]{1,0:T(8,128)S(1)}, f32[8,2176]{1,0:T(8,128)S(1)}, u32[]{:S(2)}, u32[]{:S(2)}) collective-permute-start(f32[8,2176]{1,0:T(8,128)S(1)} %get-tuple-element.14.own_ref), channel_id=1, source_target_pairs={{0,1},{1,2},{2,3},{3,4},{4,5},{5,6},{6,7},{7,8},{8,9},{9,10},{10,1... | collective-permute-start | bytes 208904 | tf_op jit(solution)/shard_map/ppermute | solution.py:396

commit v5 on v4

--- a/solution.py
+++ b/solution.py
@@ -1,4 +1,3 @@
-import functools
 import math
 
 import jax
@@ -13,7 +12,7 @@
 BLOB = 0.25
 LANES = 128
 DEPTH = 2
-EARLY = 2
+EARLY = 3
 GROUP = 16
 F32 = jnp.float32
 BF16 = jnp.bfloat16
@@ -109,7 +108,7 @@
     return [jnp.concatenate(rows, 0).astype(BF16) for rows in (rho, ab, ar, br)]
 
 
-def middle_body(rows, own_ref, left_ref, right_ref, count_hbm, slot_hbm, class_hbm, req_hbm, table_hbm, near_ref, main_ref, tail_ref, code_ref, kind_ref, kept_ref, table, count_ref, slot_ref, class_ref, req_ref, sems, win, lhs, rhs, acc, one, two, list_v, list_s, pairs, sem, flip):
+def middle_body(own_ref, left_ref, right_ref, count_hbm, slot_hbm, class_hbm, req_hbm, table_hbm, near_ref, slot_ref, req_ref, kind_ref, kept_ref, table, count_ref, class_ref, sems, win, lhs, rhs, acc, one, two, list_v, list_s, pairs, sem, flip):
     pairs_of = ((table_hbm, table), (count_hbm, count_ref), (slot_hbm, slot_ref), (class_hbm, class_ref), (req_hbm, req_ref))
     fetches = [pltpu.make_async_copy(a, b, sems.at[i]) for i, (a, b) in enumerate(pairs_of)]
     for fetch in fetches:
@@ -118,7 +117,7 @@
     for fetch in fetches:
         fetch.wait()
     keep_rows(table, kept_ref)
-    select_terms(rows, count_ref, slot_ref, class_ref, req_ref, main_ref, tail_ref, code_ref, kind_ref, flip)
+    class_terms(count_ref, class_ref, kind_ref, flip)
 
 
 def keep_rows(table, kept_ref):
@@ -152,27 +151,30 @@
             list_v[3] = jnp.where(listed > 0, (leaf_of << 6) + (source + leaf_num), -1)
     copy = pltpu.make_async_copy(list_v, list_s, sem)
     copy.start()
-    acc[...] = jnp.zeros(acc.shape, F32)
-    for place, ref in enumerate(halo):
-        for leaf in range(leaf_num):
+
+    def clear(leaf, _):
+        acc[leaf] = jnp.zeros(acc.shape[1:], F32)
+        return 0
+
+    lax.fori_loop(0, leaf_num, clear, 0)
+    lhs[leaf_num] = jnp.zeros(lhs.shape[1:], BF16)
+    copy.wait()
+    dead, seen = jnp.int32(0), 0
+    for leaf in range(leaf_num):
+        for place, ref in enumerate(halo):
             tile = ref[:, leaf * LANES : (leaf + 1) * LANES]
             win[place * leaf_num + leaf] = tile
             for k, rows in enumerate(source_rows(tile)):
                 rhs[place * leaf_num + leaf, :, k * LANES : (k + 1) * LANES] = rows
             if place == 1:
                 lhs[leaf] = target_rows(tile).T.astype(BF16)
-    lhs[leaf_num] = jnp.zeros(lhs.shape[1:], BF16)
-    copy.wait()
-
-    def scan(leaf, count):
         for place in range(list_s.shape[0]):
             for slot in range(slots):
                 code = list_s[place, slot, leaf]
-                pairs[count] = code
-                count = count + (code >= 0).astype(jnp.int32)
-        return count
-
-    count = lax.fori_loop(0, leaf_num, scan, 0)
+                pairs[dead + seen] = code
+                dead = dead + (code >> 31)
+                seen = seen + 1
+    count = dead + seen
     for i in range(3 * DEPTH):
         pairs[count + i] = leaf_num * 64
 
@@ -230,7 +232,20 @@
     return scratch[...].T
 
 
-def select_terms(rows, count_ref, slot_ref, class_ref, req_ref, main_ref, tail_ref, code_ref, kind_ref, scratch):
+def class_terms(count_ref, class_ref, kind_ref, scratch):
+    leaf_num, far_num = class_ref.shape
+    scratch[...] = jnp.zeros((LANES, LANES), F32)
+    classes = columns(scratch, class_ref[...])
+    lane = iota((far_num, LANES), 1)
+    row = iota((far_num, LANES), 0)
+    for leaf in range(leaf_num):
+        at = slice(leaf * far_num, (leaf + 1) * far_num)
+        kind = jnp.broadcast_to(classes[:far_num, leaf : leaf + 1], (far_num, LANES)).astype(jnp.int32)
+        keep = (lane % leaf_num == leaf) & (row < count_ref[leaf])
+        kind_ref[at] = jnp.where(keep, kind - lane // leaf_num, -LANES).astype(BF16)
+
+
+def slot_terms(rows, slot_ref, req_ref, main_ref, tail_ref, code_ref, scratch):
     leaf_num, far_num = slot_ref.shape
     cap, peers = req_ref.shape
     reps = LANES // leaf_num
@@ -240,31 +255,25 @@
     asked = jnp.concatenate([jnp.broadcast_to(asked[:, t : t + 1], (peers, LANES)) for t in range(cap)], 0)
     asked = asked.astype(BF16)
     slots = columns(scratch, slot_ref[...])
-    classes = columns(scratch, class_ref[...])
-    lane = iota((far_num, LANES), 1)
-    row = iota((far_num, LANES), 0)
+    slot = jnp.concatenate([jnp.broadcast_to(slots[:far_num, i : i + 1], (far_num, LANES)) for i in range(leaf_num)], 0)
+    slot = slot.astype(jnp.int32)
+    lane = iota(slot.shape, 1)
+    peer = slot // cap
+    key = (slot - peer * cap) * peers + peer - lane
+    picks = [jnp.where(key == t * peers, 1.0, 0.0).astype(BF16) for t in range(cap)]
+    local = jnp.dot(jnp.concatenate(picks, 1), asked, preferred_element_type=F32).astype(jnp.int32)
+    upper = (peer >= half).astype(jnp.int32)
+    base = (peer - upper * half) * rows
 
     def code(row):
         return jnp.where(lane == row % LANES, row // LANES, -1).astype(BF16)
 
-    for leaf in range(leaf_num):
-        at = slice(leaf * far_num, (leaf + 1) * far_num)
-        slot = jnp.broadcast_to(slots[:far_num, leaf : leaf + 1], (far_num, LANES)).astype(jnp.int32)
-        peer = slot // cap
-        key = (slot - peer * cap) * peers + peer - lane
-        picks = [jnp.where(key == t * peers, 1.0, 0.0).astype(BF16) for t in range(cap)]
-        local = jnp.dot(jnp.concatenate(picks, 1), asked, preferred_element_type=F32).astype(jnp.int32)
-        upper = (peer >= half).astype(jnp.int32)
-        base = (peer - upper * half) * rows
-        main_ref[at] = code(base + local)
-        tail_ref[at] = code(base + leaf_num + local // reps)
-        code_ref[at] = (upper + 2 * (lane // leaf_num == local % reps).astype(jnp.int32)).astype(BF16)
-        kind = jnp.broadcast_to(classes[:far_num, leaf : leaf + 1], (far_num, LANES)).astype(jnp.int32)
-        keep = (lane % leaf_num == leaf) & (row < count_ref[leaf])
-        kind_ref[at] = jnp.where(keep, kind - lane // leaf_num, -LANES).astype(BF16)
-
-
-def far_body(mom_ref, main_ref, tail_ref, code_ref, kind_ref, kept_ref, own_ref, near_ref, table_hbm, down_hbm, out_ref, table, down, pad, sums, sem):
+    main_ref[...] = code(base + local)
+    tail_ref[...] = code(base + leaf_num + local // reps)
+    code_ref[...] = (upper + 2 * (lane // leaf_num == local % reps).astype(jnp.int32)).astype(BF16)
+
+
+def far_body(mom_ref, slot_ref, req_ref, kind_ref, kept_ref, own_ref, near_ref, table_hbm, down_hbm, out_ref, main_ref, tail_ref, code_ref, flip, table, down, pad, sums, sem):
     early = kept_ref.shape[0] - GROUP
     fetch = pltpu.make_async_copy(table_hbm.at[pl.ds(early, table.shape[0])], table, sem.at[0])
     fetch_down = pltpu.make_async_copy(down_hbm, down, sem.at[1])
@@ -277,7 +286,7 @@
 
     @pl.when(lax.axis_index("patch") >= 0)
     def _():
-        groups = pad.shape[0]
+        slot_terms(mom_ref.shape[0] // (req_ref.shape[1]), slot_ref, req_ref, main_ref, tail_ref, code_ref, flip)
         half = mom_ref.shape[0] // 2
         both = jnp.concatenate([mom_ref[:half], mom_ref[half:]], 1)
         one, zero = jnp.ones((), BF16), jnp.zeros((), BF16)
@@ -297,8 +306,6 @@
         extra = width - LANES
         tails = sum(tails[i * extra : (i + 1) * extra] for i in range(LANES // extra))
         src_t = jnp.concatenate([main, tails], 0).astype(BF16)
-        lead = 2 * LANES - width
-        cols = GROUP * leaf_num
         per = cols // LANES
         hot = hots(kind_ref, groups * per, LANES // leaf_num)
         for g in range(groups):
@@ -400,12 +407,11 @@
     table = table.reshape(peers * rows, LANES)
     down_flat = down_basis.transpose(0, 2, 1, 3)
     near, *kept = call(
-        functools.partial(middle_body, rows),
+        middle_body,
         [
             (3, nodes, F32),
-            (slots, LANES, BF16),
-            (slots, LANES, BF16),
-            (slots, LANES, BF16),
+            far_slot.shape + (jnp.int32,),
+            (requests.shape[2], peers, jnp.int32),
             (slots, LANES, BF16),
             ((EARLY + 1) * GROUP, width * width, BF16),
         ],
@@ -414,9 +420,7 @@
         scratch_shapes=[
             pltpu.VMEM(transfer_table.shape, BF16),
             pltpu.SMEM(far_count.shape, jnp.int32),
-            pltpu.VMEM(far_slot.shape, jnp.int32),
             pltpu.VMEM(far_class.shape, jnp.int32),
-            pltpu.VMEM((requests.shape[2], peers), jnp.int32),
             pltpu.SemaphoreType.DMA((5,)),
             pltpu.VMEM((3 * leaf_num, 8, LANES), F32),
             pltpu.VMEM((leaf_num + 1, LANES, 48), BF16),
@@ -435,9 +439,13 @@
         far_body,
         None,
         30,
-        in_specs=[VMEM] * 8 + [HBM] * 2,
+        in_specs=[VMEM] * 7 + [HBM] * 2,
         out_shape=jax.ShapeDtypeStruct((3, nodes), F32),
         scratch_shapes=[
+            pltpu.VMEM((slots, LANES), BF16),
+            pltpu.VMEM((slots, LANES), BF16),
+            pltpu.VMEM((slots, LANES), BF16),
+            pltpu.VMEM((LANES, LANES), F32),
             pltpu.VMEM(((groups - 1 - EARLY) * GROUP, width * width), BF16),
             pltpu.VMEM(down_flat.shape, BF16),
             pltpu.VMEM((groups, 4 * LANES - width, GROUP * leaf_num), BF16),

time: 55.9 us -> 54.8 us (0.980)
  Pallas kernels: 28.2 us -> 27.1 us
    pallas_call x2, Pallas kernels: 25.3 us -> 24.2 us  [the longest x1 14 us: per_device(): call(middle_body, [(3, nodes, F32), far_slot.shape + (jnp.int32,), (reque...]
  transfers between devices with their start and end apart: 3 -> 3, of which waited for: 1 -> 1; matrix products, arithmetic and copies ran while one was open for 0% -> 0% of each run, Pallas kernels for 28% -> 26%
where the time goes in v5:
time: 54.8 us; the launch traced here: 54.5 us
  Pallas kernels  27.1 us (49%)
  starting transfers between devices  19.5 us (36%)
  waiting for transfers between devices  7.91 us (14%)
    pallas_call x1, Pallas kernels, per_device(): call(middle_body, [(3, nodes, F32), far_slot.shape + (jnp.int32,), (reque...  14 us
    all_to_all x1, starting transfers between devices, per_device(): lax.all_to_all(message, 'patch', split_axis=0, concat_axis=0, tiled=True)  10.5 us
    pallas_call x1, Pallas kernels, per_device(): call(far_body, None, 30, in_specs=[VMEM] * 7 + [HBM] * 2, out_shape=jax.S...  10.2 us
    ppermute x1, waiting for transfers between devices, per_device(): left = lax.ppermute(own, 'patch', up)  7.91 us
    ppermute x1, starting transfers between devices, per_device(): right = lax.ppermute(own, 'patch', down)  7.13 us
    pallas_call x1, Pallas kernels, per_device(): call(front_body, [(8, nodes + LANES, F32), (peers * rows, LANES, BF16)],...  2.92 us
    ppermute x1, starting transfers between devices, per_device(): left = lax.ppermute(own, 'patch', up)  1.92 us
  transfers between devices with their start and end apart: 3, of which 1 were waited for; matrix products, arithmetic and copies ran while one was open for 0% of the time, Pallas kernels for 26%

profile of v5, /device:TPU:8, one launch (start us, length us, event | category | flops | bytes accessed | tf_op | source)
XLA Modules:
  0.0 54.5 jit_solution(11520311164668876429)
XLA Ops:
  0.0 2.9 %shard_map.109 = (f32[8,2176]{1,0:T(8,128)S(1)}, bf16[2304,128]{1,0:T(8,128)(2,1)}) custom-call(f32[3,2048]{1,0:T(4,128)} %pos_hbm.1, f32[3,2048]{1,0:T(4,128)} %dens_hbm.1, s32[8,16]{1,0:T(8,128)} %bitcast.10, s32[1,16]{1,0:T(1,128)} %bitcast.12, bf16[16,144,384]{2,1,0:T(8,128)(2,1)} %up_hbm.1), custom_call_target="tpu_custom_call" | custom-call | tf_op jit(solution)/shard_map/pallas_call | solution.py:389
  2.9 10.5 %all-to-all-start = ((bf16[128,9,2,128]{3,2,1,0:T(2,128)(2,1)}), bf16[128,9,2,128]{3,2,1,0:T(2,128)(2,1)S(1)}, u32[]{:S(2)}, u32[]{:S(2)}) async-start(bf16[128,9,2,128]{3,2,1,0:T(2,128)(2,1)} %bitcast.2), calls=%async_computation | async-start | bytes 1179648 | tf_op jit(solution)/shard_map/all_to_all | solution.py:406
  13.4 7.1 %collective-permute-start.1 = (f32[8,2176]{1,0:T(8,128)S(1)}, f32[8,2176]{1,0:T(8,128)S(1)}, u32[]{:S(2)}, u32[]{:S(2)}) collective-permute-start(f32[8,2176]{1,0:T(8,128)S(1)} %get-tuple-element.13.own_ref), channel_id=1, source_target_pairs={{1,0},{2,1},{3,2},{4,3},{5,4},{6,5},{7,6},{8,7},{9,8},{10,9},{11,1... | collective-permute-start | bytes 208904 | tf_op jit(solution)/shard_map/ppermute | solution.py:404
  20.5 1.9 %collective-permute-start = (f32[8,2176]{1,0:T(8,128)S(1)}, f32[8,2176]{1,0:T(8,128)S(1)}, u32[]{:S(2)}, u32[]{:S(2)}) collective-permute-start(f32[8,2176]{1,0:T(8,128)S(1)} %get-tuple-element.13.own_ref), channel_id=1, source_target_pairs={{0,1},{1,2},{2,3},{3,4},{4,5},{5,6},{6,7},{7,8},{8,9},{9,10},{10,1... | collective-permute-start | bytes 208904 | tf_op jit(solution)/shard_map/ppermute | solution.py:403
  22.5 0.0 collective-permute-done.1.right_ref
  22.5 7.9 %collective-permute-done.left_ref = f32[8,2176]{1,0:T(8,128)S(1)} collective-permute-done((f32[8,2176]{1,0:T(8,128)S(1)}, f32[8,2176]{1,0:T(8,128)S(1)}, u32[]{:S(2)}, u32[]{:S(2)}) %collective-permute-start) | collective-permute-done | bytes 69664 | tf_op jit(solution)/shard_map/ppermute | solution.py:403
  30.4 14.0 %shard_map.110 = (f32[3,2048]{1,0:T(4,128)S(1)}, s32[16,32]{1,0:T(8,128)S(1)}, s32[4,128]{1,0:T(4,128)S(1)}, bf16[512,128]{1,0:T(8,128)(2,1)S(1)}, bf16[64,20736]{1,0:T(8,128)(2,1)S(1)}) custom-call(f32[8,2176]{1,0:T(8,128)S(1)} %get-tuple-element.13.own_ref, f32[8,2176]{1,0:T(8,128)S(1)} %collective-permute-done.left_ref, ...), custom_call_target="tpu_custom_call" | custom-call | tf_op jit(solution)/shard_map/pallas_call | solution.py:409
  44.4 0.0 all-to-all-done
  44.4 10.2 %shard_map.111 = f32[3,2048]{1,0:T(4,128)} custom-call(bf16[2304,128]{1,0:T(8,128)(2,1)S(1)} %bitcast.8, s32[16,32]{1,0:T(8,128)S(1)} %get-tuple-element.14.slot_ref, s32[4,128]{1,0:T(4,128)S(1)} %get-tuple-element.15.req_ref, bf16[512,128]{1,0:T(8,128)(2,1)S(1)} %get-tuple-element.16.kind_ref, bf16[64,20736]{1,0:T(8,128)(2,1)S(1)} %get-tuple-element.17.kept_ref, ...), custom_call_target="tpu_custom_call" | custom-call | tf_op jit(solution)/shard_map/pallas_call | solution.py:438
Async XLA Ops:
  2.9 41.4 %all-to-all-start = ((bf16[128,9,2,128]{3,2,1,0:T(2,128)(2,1)}), bf16[128,9,2,128]{3,2,1,0:T(2,128)(2,1)S(1)}, u32[]{:S(2)}, u32[]{:S(2)}) async-start(bf16[128,9,2,128]{3,2,1,0:T(2,128)(2,1)} %bitcast.2), calls=%async_computation | async-start | bytes 1179648 | tf_op jit(solution)/shard_map/all_to_all | solution.py:406
  13.4 9.1 %collective-permute-start.1 = (f32[8,2176]{1,0:T(8,128)S(1)}, f32[8,2176]{1,0:T(8,128)S(1)}, u32[]{:S(2)}, u32[]{:S(2)}) collective-permute-start(f32[8,2176]{1,0:T(8,128)S(1)} %get-tuple-element.13.own_ref), channel_id=1, source_target_pairs={{1,0},{2,1},{3,2},{4,3},{5,4},{6,5},{7,6},{8,7},{9,8},{10,9},{11,1... | collective-permute-start | bytes 208904 | tf_op jit(solution)/shard_map/ppermute | solution.py:404
  20.5 9.8 %collective-permute-start = (f32[8,2176]{1,0:T(8,128)S(1)}, f32[8,2176]{1,0:T(8,128)S(1)}, u32[]{:S(2)}, u32[]{:S(2)}) collective-permute-start(f32[8,2176]{1,0:T(8,128)S(1)} %get-tuple-element.13.own_ref), channel_id=1, source_target_pairs={{0,1},{1,2},{2,3},{3,4},{4,5},{5,6},{6,7},{7,8},{8,9},{9,10},{10,1... | collective-permute-start | bytes 208904 | tf_op jit(solution)/shard_map/ppermute | solution.py:403

commit v6 on v5

--- a/solution.py
+++ b/solution.py
@@ -11,8 +11,8 @@
 KERNEL = 1.0 / (8.0 * math.pi)
 BLOB = 0.25
 LANES = 128
-DEPTH = 2
-EARLY = 3
+DEPTH = 3
+EARLY = 2
 GROUP = 16
 F32 = jnp.float32
 BF16 = jnp.bfloat16
@@ -108,12 +108,12 @@
     return [jnp.concatenate(rows, 0).astype(BF16) for rows in (rho, ab, ar, br)]
 
 
-def middle_body(own_ref, left_ref, right_ref, count_hbm, slot_hbm, class_hbm, req_hbm, table_hbm, near_ref, slot_ref, req_ref, kind_ref, kept_ref, table, count_ref, class_ref, sems, win, lhs, rhs, acc, one, two, list_v, list_s, pairs, sem, flip):
+def middle_body(own_ref, left_ref, right_ref, count_hbm, slot_hbm, class_hbm, req_hbm, table_hbm, near_ref, slot_ref, req_ref, kind_ref, kept_ref, table, count_ref, class_ref, sems, win, lhs, rhs, acc, list_v, list_s, pairs, sem, flip):
     pairs_of = ((table_hbm, table), (count_hbm, count_ref), (slot_hbm, slot_ref), (class_hbm, class_ref), (req_hbm, req_ref))
     fetches = [pltpu.make_async_copy(a, b, sems.at[i]) for i, (a, b) in enumerate(pairs_of)]
     for fetch in fetches:
         fetch.start()
-    near_terms(own_ref, left_ref, right_ref, near_ref, win, lhs, rhs, acc, one, two, list_v, list_s, pairs, sem)
+    near_terms(own_ref, left_ref, right_ref, near_ref, win, lhs, rhs, acc, list_v, list_s, pairs, sem)
     for fetch in fetches:
         fetch.wait()
     keep_rows(table, kept_ref)
@@ -135,7 +135,7 @@
         kept_ref[first:, cols] = both.astype(BF16)
 
 
-def near_terms(own_ref, left_ref, right_ref, near_ref, win, lhs, rhs, acc, one, two, list_v, list_s, pairs, sem):
+def near_terms(own_ref, left_ref, right_ref, near_ref, win, lhs, rhs, acc, list_v, list_s, pairs, sem):
     leaf_num = acc.shape[0] - 1
     nodes = leaf_num * LANES
     slots = list_v.shape[1]
@@ -167,7 +167,9 @@
             for k, rows in enumerate(source_rows(tile)):
                 rhs[place * leaf_num + leaf, :, k * LANES : (k + 1) * LANES] = rows
             if place == 1:
-                lhs[leaf] = target_rows(tile).T.astype(BF16)
+                rows = target_rows(tile)
+                rows = jnp.concatenate([rows, jnp.zeros((LANES - rows.shape[0], LANES), F32)], 0)
+                lhs[leaf] = rows.T.astype(BF16)
         for place in range(list_s.shape[0]):
             for slot in range(slots):
                 code = list_s[place, slot, leaf]
@@ -178,17 +180,24 @@
     for i in range(3 * DEPTH):
         pairs[count + i] = leaf_num * 64
 
-    def products(at, buf):
+    def products(at, bufs, register):
         pair = pairs[at]
-        buf[...] = jnp.dot(lhs[pair >> 6], rhs[pair & 63], preferred_element_type=F32)
-
-    def add_terms(at, buf):
+        left = jnp.concatenate([lhs[pair >> 6], jnp.zeros((LANES, LANES), BF16)], 1)
+        for unit, buf in enumerate(bufs):
+            right = rhs[pair & 63, :, unit * 2 * LANES : (unit + 1) * 2 * LANES]
+            right = jnp.concatenate([right, jnp.zeros((2 * LANES - right.shape[0], 2 * LANES), BF16)], 0)
+            pltpu.matmul_push_rhs(right, staging_register=register, mxu_index=unit)
+            pltpu.matmul_acc_lhs(buf, left, load_staged_rhs=register)
+
+    def add_terms(at, bufs):
         pair = pairs[at]
         target, source = pair >> 6, pair & 63
         row = [jnp.broadcast_to(win[source, k : k + 1], (8, LANES)) for k in range(6)]
+        first, second = [pltpu.matmul_pop(buf) for buf in bufs]
         for part in range(LANES // 8):
             i = slice(part * 8, part * 8 + 8)
-            rho_sq, ab, ar, br = [buf[i, k * LANES : (k + 1) * LANES] for k in range(4)]
+            rho_sq, ab = first[i, :LANES], first[i, LANES:]
+            ar, br = second[i, :LANES], second[i, LANES:]
             inv_one = lax.rsqrt(rho_sq)
             inv_two = inv_one * inv_one
             inv_three = inv_two * inv_one
@@ -199,22 +208,32 @@
             for k in range(3):
                 acc[target, 2 + k, i] += row[3 + k] * ar + row[k] * coef
 
-    for i in range(DEPTH):
-        products(i, one.at[i])
-
-    def blocks(step, _):
-        first = step * (2 * DEPTH)
+    def run(*bufs):
+        bufs = [bufs[i : i + 2] for i in range(0, 4 * DEPTH, 2)]
+        for pair in bufs:
+            for buf in pair:
+                pltpu.matmul_pop(buf)
         for i in range(DEPTH):
-            products(first + DEPTH + i, two.at[i])
-        for i in range(DEPTH):
-            add_terms(first + i, one.at[i])
-        for i in range(DEPTH):
-            products(first + 2 * DEPTH + i, one.at[i])
-        for i in range(DEPTH):
-            add_terms(first + DEPTH + i, two.at[i])
-        return 0
-
-    lax.fori_loop(0, (count + 2 * DEPTH - 1) // (2 * DEPTH), blocks, 0)
+            products(i, bufs[i], i % 2)
+
+        def blocks(step, _):
+            start = step * (2 * DEPTH)
+            for i in range(DEPTH):
+                products(start + DEPTH + i, bufs[DEPTH + i], i % 2)
+            for i in range(DEPTH):
+                add_terms(start + i, bufs[i])
+            for i in range(DEPTH):
+                products(start + 2 * DEPTH + i, bufs[i], i % 2)
+            for i in range(DEPTH):
+                add_terms(start + DEPTH + i, bufs[DEPTH + i])
+            return 0
+
+        lax.fori_loop(0, (count + 2 * DEPTH - 1) // (2 * DEPTH), blocks, 0)
+        for pair in bufs[:DEPTH]:
+            for buf in pair:
+                pltpu.matmul_pop(buf)
+
+    pl.run_scoped(run, *[pltpu.ACC(i % 2)((LANES, 2 * LANES), F32) for i in range(4 * DEPTH)])
     lane = iota((LANES, LANES), 1)
     for leaf in range(leaf_num):
         flat = jnp.zeros((LANES, LANES), F32)
@@ -423,11 +442,9 @@
             pltpu.VMEM(far_class.shape, jnp.int32),
             pltpu.SemaphoreType.DMA((5,)),
             pltpu.VMEM((3 * leaf_num, 8, LANES), F32),
-            pltpu.VMEM((leaf_num + 1, LANES, 48), BF16),
+            pltpu.VMEM((leaf_num + 1, LANES, LANES), BF16),
             pltpu.VMEM((3 * leaf_num, 48, 4 * LANES), BF16),
             pltpu.VMEM((leaf_num + 1, 5, LANES, LANES), F32),
-            pltpu.VMEM((DEPTH, LANES, 4 * LANES), F32),
-            pltpu.VMEM((DEPTH, LANES, 4 * LANES), F32),
             pltpu.VMEM((4, slot_num, LANES), jnp.int32),
             pltpu.SMEM((4, slot_num, LANES), jnp.int32),
             pltpu.SMEM((4 * leaf_num * slot_num + 3 * DEPTH,), jnp.int32),

time: 54.8 us -> 52.6 us (0.960)
  Pallas kernels: 27.1 us -> 25 us
    pallas_call x1, Pallas kernels: 14 us -> 11.8 us  [per_device(): call(middle_body, [(3, nodes, F32), far_slot.shape + (jnp.int32,), (reque...]
  transfers between devices with their start and end apart: 3 -> 3, of which waited for: 1 -> 1; matrix products, arithmetic and copies ran while one was open for 0% -> 0% of each run, Pallas kernels for 26% -> 23%
where the time goes in v6:
time: 52.6 us; the launch traced here: 52.4 us
  Pallas kernels  25 us (48%)
  starting transfers between devices  19.5 us (37%)
  waiting for transfers between devices  7.91 us (15%)
    pallas_call x1, Pallas kernels, per_device(): call(middle_body, [(3, nodes, F32), far_slot.shape + (jnp.int32,), (reque...  11.8 us
    all_to_all x1, starting transfers between devices, per_device(): lax.all_to_all(message, 'patch', split_axis=0, concat_axis=0, tiled=True)  10.5 us
    pallas_call x1, Pallas kernels, per_device(): call(far_body, None, 30, in_specs=[VMEM] * 7 + [HBM] * 2, out_shape=jax.S...  10.2 us
    ppermute x1, waiting for transfers between devices, per_device(): left = lax.ppermute(own, 'patch', up)  7.91 us
    ppermute x1, starting transfers between devices, per_device(): right = lax.ppermute(own, 'patch', down)  7.13 us
    pallas_call x1, Pallas kernels, per_device(): call(front_body, [(8, nodes + LANES, F32), (peers * rows, LANES, BF16)],...  2.92 us
    ppermute x1, starting transfers between devices, per_device(): left = lax.ppermute(own, 'patch', up)  1.92 us
  transfers between devices with their start and end apart: 3, of which 1 were waited for; matrix products, arithmetic and copies ran while one was open for 0% of the time, Pallas kernels for 23%

profile of v6, /device:TPU:8, one launch (start us, length us, event | category | flops | bytes accessed | tf_op | source)
XLA Modules:
  0.0 52.4 jit_solution(3513116993171324397)
XLA Ops:
  0.0 2.9 %shard_map.109 = (f32[8,2176]{1,0:T(8,128)S(1)}, bf16[2304,128]{1,0:T(8,128)(2,1)}) custom-call(f32[3,2048]{1,0:T(4,128)} %pos_hbm.1, f32[3,2048]{1,0:T(4,128)} %dens_hbm.1, s32[8,16]{1,0:T(8,128)} %bitcast.10, s32[1,16]{1,0:T(1,128)} %bitcast.12, bf16[16,144,384]{2,1,0:T(8,128)(2,1)} %up_hbm.1), custom_call_target="tpu_custom_call" | custom-call | tf_op jit(solution)/shard_map/pallas_call | solution.py:408
  2.9 10.5 %all-to-all-start = ((bf16[128,9,2,128]{3,2,1,0:T(2,128)(2,1)}), bf16[128,9,2,128]{3,2,1,0:T(2,128)(2,1)S(1)}, u32[]{:S(2)}, u32[]{:S(2)}) async-start(bf16[128,9,2,128]{3,2,1,0:T(2,128)(2,1)} %bitcast.2), calls=%async_computation | async-start | bytes 1179648 | tf_op jit(solution)/shard_map/all_to_all | solution.py:425
  13.4 7.1 %collective-permute-start.1 = (f32[8,2176]{1,0:T(8,128)S(1)}, f32[8,2176]{1,0:T(8,128)S(1)}, u32[]{:S(2)}, u32[]{:S(2)}) collective-permute-start(f32[8,2176]{1,0:T(8,128)S(1)} %get-tuple-element.13.own_ref), channel_id=1, source_target_pairs={{1,0},{2,1},{3,2},{4,3},{5,4},{6,5},{7,6},{8,7},{9,8},{10,9},{11,1... | collective-permute-start | bytes 208904 | tf_op jit(solution)/shard_map/ppermute | solution.py:423
  20.5 1.9 %collective-permute-start = (f32[8,2176]{1,0:T(8,128)S(1)}, f32[8,2176]{1,0:T(8,128)S(1)}, u32[]{:S(2)}, u32[]{:S(2)}) collective-permute-start(f32[8,2176]{1,0:T(8,128)S(1)} %get-tuple-element.13.own_ref), channel_id=1, source_target_pairs={{0,1},{1,2},{2,3},{3,4},{4,5},{5,6},{6,7},{7,8},{8,9},{9,10},{10,1... | collective-permute-start | bytes 208904 | tf_op jit(solution)/shard_map/ppermute | solution.py:422
  22.5 0.0 collective-permute-done.1.right_ref
  22.5 7.9 %collective-permute-done.left_ref = f32[8,2176]{1,0:T(8,128)S(1)} collective-permute-done((f32[8,2176]{1,0:T(8,128)S(1)}, f32[8,2176]{1,0:T(8,128)S(1)}, u32[]{:S(2)}, u32[]{:S(2)}) %collective-permute-start) | collective-permute-done | bytes 69664 | tf_op jit(solution)/shard_map/ppermute | solution.py:422
  30.4 11.8 %shard_map.110 = (f32[3,2048]{1,0:T(4,128)S(1)}, s32[16,32]{1,0:T(8,128)S(1)}, s32[4,128]{1,0:T(4,128)S(1)}, bf16[512,128]{1,0:T(8,128)(2,1)S(1)}, bf16[48,20736]{1,0:T(8,128)(2,1)S(1)}) custom-call(f32[8,2176]{1,0:T(8,128)S(1)} %get-tuple-element.13.own_ref, f32[8,2176]{1,0:T(8,128)S(1)} %collective-permute-done.left_ref, ...), custom_call_target="tpu_custom_call" | custom-call | tf_op jit(solution)/shard_map/pallas_call | solution.py:428
  42.2 0.0 all-to-all-done
  42.2 10.2 %shard_map.111 = f32[3,2048]{1,0:T(4,128)} custom-call(bf16[2304,128]{1,0:T(8,128)(2,1)S(1)} %bitcast.8, s32[16,32]{1,0:T(8,128)S(1)} %get-tuple-element.14.slot_ref, s32[4,128]{1,0:T(4,128)S(1)} %get-tuple-element.15.req_ref, bf16[512,128]{1,0:T(8,128)(2,1)S(1)} %get-tuple-element.16.kind_ref, bf16[48,20736]{1,0:T(8,128)(2,1)S(1)} %get-tuple-element.17.kept_ref, ...), custom_call_target="tpu_custom_call" | custom-call | tf_op jit(solution)/shard_map/pallas_call | solution.py:455
Async XLA Ops:
  2.9 39.3 %all-to-all-start = ((bf16[128,9,2,128]{3,2,1,0:T(2,128)(2,1)}), bf16[128,9,2,128]{3,2,1,0:T(2,128)(2,1)S(1)}, u32[]{:S(2)}, u32[]{:S(2)}) async-start(bf16[128,9,2,128]{3,2,1,0:T(2,128)(2,1)} %bitcast.2), calls=%async_computation | async-start | bytes 1179648 | tf_op jit(solution)/shard_map/all_to_all | solution.py:425
  13.4 9.1 %collective-permute-start.1 = (f32[8,2176]{1,0:T(8,128)S(1)}, f32[8,2176]{1,0:T(8,128)S(1)}, u32[]{:S(2)}, u32[]{:S(2)}) collective-permute-start(f32[8,2176]{1,0:T(8,128)S(1)} %get-tuple-element.13.own_ref), channel_id=1, source_target_pairs={{1,0},{2,1},{3,2},{4,3},{5,4},{6,5},{7,6},{8,7},{9,8},{10,9},{11,1... | collective-permute-start | bytes 208904 | tf_op jit(solution)/shard_map/ppermute | solution.py:423
  20.5 9.8 %collective-permute-start = (f32[8,2176]{1,0:T(8,128)S(1)}, f32[8,2176]{1,0:T(8,128)S(1)}, u32[]{:S(2)}, u32[]{:S(2)}) collective-permute-start(f32[8,2176]{1,0:T(8,128)S(1)} %get-tuple-element.13.own_ref), channel_id=1, source_target_pairs={{0,1},{1,2},{2,3},{3,4},{4,5},{5,6},{6,7},{7,8},{8,9},{9,10},{10,1... | collective-permute-start | bytes 208904 | tf_op jit(solution)/shard_map/ppermute | solution.py:422

commit v7 on v6

--- a/solution.py
+++ b/solution.py
@@ -22,8 +22,17 @@
     return lax.broadcasted_iota(jnp.int32, shape, dim)
 
 
+def quotient(x, n):
+    return x >> (n.bit_length() - 1) if n & (n - 1) == 0 else x // n
+
+
+def remainder(x, n):
+    return x & (n - 1) if n & (n - 1) == 0 else x % n
+
+
 def front_body(pos_hbm, dens_hbm, src_hbm, count_hbm, up_hbm, own_ref, out_ref, pos_ref, dens_ref, src_ref, count_ref, up_ref, sem):
-    refs = ((pos_hbm, pos_ref), (dens_hbm, dens_ref), (src_hbm, src_ref), (count_hbm, count_ref), (up_hbm, up_ref))
+    refs = [(pos_hbm, pos_ref), (dens_hbm, dens_ref), (src_hbm, src_ref), (count_hbm, count_ref)]
+    refs += [(up_hbm.at[pl.ds(i, 4)], up_ref.at[pl.ds(i, 4)]) for i in range(0, up_ref.shape[0], 4)]
     copies = [pltpu.make_async_copy(a, b, sem.at[i]) for i, (a, b) in enumerate(refs)]
     for copy in copies:
         copy.start()
@@ -38,10 +47,11 @@
     own_ref[3:6, :nodes] = dens_ref[...]
     live = iota((slots, leaf_num), 0) < count_ref[...]
     own_ref[:, nodes : nodes + leaf_num] = jnp.where(live, src_ref[...] + 1, 0).astype(F32)
-    copies[4].wait()
     lane = iota((width, LANES), 1)
     cols = jnp.zeros((width, LANES), F32)
     for leaf in range(leaf_num):
+        if leaf % 4 == 0:
+            copies[4 + leaf // 4].wait()
         total = None
         for comp in range(3):
             row = dens_ref[comp : comp + 1, leaf * LANES : (leaf + 1) * LANES]
@@ -260,8 +270,8 @@
     for leaf in range(leaf_num):
         at = slice(leaf * far_num, (leaf + 1) * far_num)
         kind = jnp.broadcast_to(classes[:far_num, leaf : leaf + 1], (far_num, LANES)).astype(jnp.int32)
-        keep = (lane % leaf_num == leaf) & (row < count_ref[leaf])
-        kind_ref[at] = jnp.where(keep, kind - lane // leaf_num, -LANES).astype(BF16)
+        keep = (remainder(lane, leaf_num) == leaf) & (row < count_ref[leaf])
+        kind_ref[at] = jnp.where(keep, kind - quotient(lane, leaf_num), -LANES).astype(BF16)
 
 
 def slot_terms(rows, slot_ref, req_ref, main_ref, tail_ref, code_ref, scratch):
@@ -277,7 +287,7 @@
     slot = jnp.concatenate([jnp.broadcast_to(slots[:far_num, i : i + 1], (far_num, LANES)) for i in range(leaf_num)], 0)
     slot = slot.astype(jnp.int32)
     lane = iota(slot.shape, 1)
-    peer = slot // cap
+    peer = quotient(slot, cap)
     key = (slot - peer * cap) * peers + peer - lane
     picks = [jnp.where(key == t * peers, 1.0, 0.0).astype(BF16) for t in range(cap)]
     local = jnp.dot(jnp.concatenate(picks, 1), asked, preferred_element_type=F32).astype(jnp.int32)
@@ -285,11 +295,11 @@
     base = (peer - upper * half) * rows
 
     def code(row):
-        return jnp.where(lane == row % LANES, row // LANES, -1).astype(BF16)
+        return jnp.where(lane == remainder(row, LANES), quotient(row, LANES), -1).astype(BF16)
 
     main_ref[...] = code(base + local)
-    tail_ref[...] = code(base + leaf_num + local // reps)
-    code_ref[...] = (upper + 2 * (lane // leaf_num == local % reps).astype(jnp.int32)).astype(BF16)
+    tail_ref[...] = code(base + leaf_num + quotient(local, reps))
+    code_ref[...] = (upper + 2 * (quotient(lane, leaf_num) == remainder(local, reps)).astype(jnp.int32)).astype(BF16)
 
 
 def far_body(mom_ref, slot_ref, req_ref, kind_ref, kept_ref, own_ref, near_ref, table_hbm, down_hbm, out_ref, main_ref, tail_ref, code_ref, flip, table, down, pad, sums, sem):
@@ -338,7 +348,7 @@
     period = LANES // step
     tiles = period + 1
     blocks = width // period
-    same = iota((blocks, GROUP, cols), 2) // leaf_num == iota((blocks, GROUP, cols), 1)
+    same = quotient(iota((blocks, GROUP, cols), 2), leaf_num) == iota((blocks, GROUP, cols), 1)
     for r in range(period):
         acc = None
         for g in range(groups):
@@ -355,7 +365,7 @@
         acc = jnp.sum(acc, axis=1)
         for h in range(cols // LANES):
             sums[h, pl.ds(r, blocks, stride=period), :] = acc[:, h * LANES : (h + 1) * LANES]
-    fold = jnp.where(iota((leaf_num, cols), 1) % leaf_num == iota((leaf_num, cols), 0), 1.0, 0.0)
+    fold = jnp.where(remainder(iota((leaf_num, cols), 1), leaf_num) == iota((leaf_num, cols), 0), 1.0, 0.0)
     whole = jnp.concatenate([sums[h] for h in range(cols // LANES)], 1)
     expansion = lax.dot_general(fold, whole, (((1,), (1,)), ((), ())), precision=lax.Precision.HIGHEST, preferred_element_type=F32)
     fetch_down.wait()
@@ -402,7 +412,7 @@
     classes = transfer_table.shape[0]
     groups = -(-classes // GROUP)
     rows = leaf_num * width // LANES
-    up = [(i, i + 1) for i in range(peers - 1)]
+    up = [(i, (i + 1) % peers) for i in range(peers)]
     down = [(j, i) for i, j in up]
     slots = leaf_num * far_num
     own, message = call(
@@ -416,7 +426,7 @@
             pltpu.VMEM((slot_num, leaf_num), jnp.int32),
             pltpu.VMEM((1, leaf_num), jnp.int32),
             pltpu.VMEM(up_basis.shape, BF16),
-            pltpu.SemaphoreType.DMA((5,)),
+            pltpu.SemaphoreType.DMA((4 + leaf_num // 4,)),
         ],
     )(*[held(x, pltpu.HBM) for x in (positions, densities, near_src.T, near_count[None], up_basis)])
     left = lax.ppermute(own, "patch", up)

time: 52.6 us -> 50.3 us (0.956)
  the two profiles are of different devices: /device:TPU:8 before, /device:TPU:0 now
where the time goes in v7:
time: 50.3 us; the launch traced here: 50.2 us
  Pallas kernels  22.7 us (45%)
  starting transfers between devices  18.3 us (36%)
  waiting for transfers between devices  9.16 us (18%)
    all_to_all x1, starting transfers between devices, per_device(): lax.all_to_all(message, 'patch', split_axis=0, concat_axis=0, tiled=True)  11.2 us
    pallas_call x1, Pallas kernels, per_device(): call(middle_body, [(3, nodes, F32), far_slot.shape + (jnp.int32,), (reque...  10.2 us
    pallas_call x1, Pallas kernels, per_device(): call(far_body, None, 30, in_specs=[VMEM] * 7 + [HBM] * 2, out_shape=jax.S...  9.78 us
    ppermute x1, waiting for transfers between devices, per_device(): left = lax.ppermute(own, 'patch', up)  7.22 us
    ppermute x1, starting transfers between devices, per_device(): right = lax.ppermute(own, 'patch', down)  7.1 us
    pallas_call x1, Pallas kernels, per_device(): call(front_body, [(8, nodes + LANES, F32), (peers * rows, LANES, BF16)],...  2.69 us
    ppermute x1, waiting for transfers between devices, per_device(): right = lax.ppermute(own, 'patch', down)  1.94 us
  transfers between devices with their start and end apart: 3, of which 2 were waited for; matrix products, arithmetic and copies ran while one was open for 0% of the time, Pallas kernels for 20%

profile of v7, /device:TPU:0, one launch (start us, length us, event | category | flops | bytes accessed | tf_op | source)
XLA Modules:
  0.0 50.2 jit_solution(990693497725150537)
XLA Ops:
  0.0 2.7 %shard_map.109 = (f32[8,2176]{1,0:T(8,128)S(1)}, bf16[2304,128]{1,0:T(8,128)(2,1)}) custom-call(f32[3,2048]{1,0:T(4,128)} %pos_hbm.1, f32[3,2048]{1,0:T(4,128)} %dens_hbm.1, s32[8,16]{1,0:T(8,128)} %bitcast.10, s32[1,16]{1,0:T(1,128)} %bitcast.12, bf16[16,144,384]{2,1,0:T(8,128)(2,1)} %up_hbm.1), custom_call_target="tpu_custom_call" | custom-call | tf_op jit(solution)/shard_map/pallas_call | solution.py:418
  2.7 11.2 %all-to-all-start = ((bf16[128,9,2,128]{3,2,1,0:T(2,128)(2,1)}), bf16[128,9,2,128]{3,2,1,0:T(2,128)(2,1)S(1)}, u32[]{:S(2)}, u32[]{:S(2)}) async-start(bf16[128,9,2,128]{3,2,1,0:T(2,128)(2,1)} %bitcast.2), calls=%async_computation | async-start | bytes 1179648 | tf_op jit(solution)/shard_map/all_to_all | solution.py:435
  13.9 7.1 %collective-permute-start.1 = (f32[8,2176]{1,0:T(8,128)S(1)}, f32[8,2176]{1,0:T(8,128)S(1)}, u32[]{:S(2)}, u32[]{:S(2)}) collective-permute-start(f32[8,2176]{1,0:T(8,128)S(1)} %get-tuple-element.13.own_ref), channel_id=1, source_target_pairs={{1,0},{2,1},{3,2},{4,3},{5,4},{6,5},{7,6},{8,7},{9,8},{10,9},{11,1... | collective-permute-start | bytes 208904 | tf_op jit(solution)/shard_map/ppermute | solution.py:433
  21.0 0.0 collective-permute-start
  21.0 1.9 %collective-permute-done.1.right_ref = f32[8,2176]{1,0:T(8,128)S(1)} collective-permute-done((f32[8,2176]{1,0:T(8,128)S(1)}, f32[8,2176]{1,0:T(8,128)S(1)}, u32[]{:S(2)}, u32[]{:S(2)}) %collective-permute-start.1) | collective-permute-done | bytes 69664 | tf_op jit(solution)/shard_map/ppermute | solution.py:433
  22.9 7.2 %collective-permute-done.left_ref = f32[8,2176]{1,0:T(8,128)S(1)} collective-permute-done((f32[8,2176]{1,0:T(8,128)S(1)}, f32[8,2176]{1,0:T(8,128)S(1)}, u32[]{:S(2)}, u32[]{:S(2)}) %collective-permute-start) | collective-permute-done | bytes 69664 | tf_op jit(solution)/shard_map/ppermute | solution.py:432
  30.2 10.2 %shard_map.110 = (f32[3,2048]{1,0:T(4,128)S(1)}, s32[16,32]{1,0:T(8,128)S(1)}, s32[4,128]{1,0:T(4,128)S(1)}, bf16[512,128]{1,0:T(8,128)(2,1)S(1)}, bf16[48,20736]{1,0:T(8,128)(2,1)S(1)}) custom-call(f32[8,2176]{1,0:T(8,128)S(1)} %get-tuple-element.13.own_ref, f32[8,2176]{1,0:T(8,128)S(1)} %collective-permute-done.left_ref, ...), custom_call_target="tpu_custom_call" | custom-call | tf_op jit(solution)/shard_map/pallas_call | solution.py:438
  40.4 0.0 all-to-all-done
  40.4 9.8 %shard_map.111 = f32[3,2048]{1,0:T(4,128)} custom-call(bf16[2304,128]{1,0:T(8,128)(2,1)S(1)} %bitcast.8, s32[16,32]{1,0:T(8,128)S(1)} %get-tuple-element.14.slot_ref, s32[4,128]{1,0:T(4,128)S(1)} %get-tuple-element.15.req_ref, bf16[512,128]{1,0:T(8,128)(2,1)S(1)} %get-tuple-element.16.kind_ref, bf16[48,20736]{1,0:T(8,128)(2,1)S(1)} %get-tuple-element.17.kept_ref, ...), custom_call_target="tpu_custom_call" | custom-call | tf_op jit(solution)/shard_map/pallas_call | solution.py:465
Async XLA Ops:
  2.7 37.7 %all-to-all-start = ((bf16[128,9,2,128]{3,2,1,0:T(2,128)(2,1)}), bf16[128,9,2,128]{3,2,1,0:T(2,128)(2,1)S(1)}, u32[]{:S(2)}, u32[]{:S(2)}) async-start(bf16[128,9,2,128]{3,2,1,0:T(2,128)(2,1)} %bitcast.2), calls=%async_computation | async-start | bytes 1179648 | tf_op jit(solution)/shard_map/all_to_all | solution.py:435
  13.9 9.0 %collective-permute-start.1 = (f32[8,2176]{1,0:T(8,128)S(1)}, f32[8,2176]{1,0:T(8,128)S(1)}, u32[]{:S(2)}, u32[]{:S(2)}) collective-permute-start(f32[8,2176]{1,0:T(8,128)S(1)} %get-tuple-element.13.own_ref), channel_id=1, source_target_pairs={{1,0},{2,1},{3,2},{4,3},{5,4},{6,5},{7,6},{8,7},{9,8},{10,9},{11,1... | collective-permute-start | bytes 208904 | tf_op jit(solution)/shard_map/ppermute | solution.py:433
  21.0 9.2 %collective-permute-start = (f32[8,2176]{1,0:T(8,128)S(1)}, f32[8,2176]{1,0:T(8,128)S(1)}, u32[]{:S(2)}, u32[]{:S(2)}) collective-permute-start(f32[8,2176]{1,0:T(8,128)S(1)} %get-tuple-element.13.own_ref), channel_id=1, source_target_pairs={{0,1},{1,2},{2,3},{3,4},{4,5},{5,6},{6,7},{7,8},{8,9},{9,10},{10,1... | collective-permute-start | bytes 208904 | tf_op jit(solution)/shard_map/ppermute | solution.py:432

commit v8 on v7

--- a/solution.py
+++ b/solution.py
@@ -118,12 +118,12 @@
     return [jnp.concatenate(rows, 0).astype(BF16) for rows in (rho, ab, ar, br)]
 
 
-def middle_body(own_ref, left_ref, right_ref, count_hbm, slot_hbm, class_hbm, req_hbm, table_hbm, near_ref, slot_ref, req_ref, kind_ref, kept_ref, table, count_ref, class_ref, sems, win, lhs, rhs, acc, list_v, list_s, pairs, sem, flip):
+def middle_body(own_ref, pair_ref, next_ref, count_hbm, slot_hbm, class_hbm, req_hbm, table_hbm, near_ref, slot_ref, req_ref, kind_ref, kept_ref, table, count_ref, class_ref, sems, win, lhs, rhs, acc, list_v, list_s, pairs, sem, flip):
     pairs_of = ((table_hbm, table), (count_hbm, count_ref), (slot_hbm, slot_ref), (class_hbm, class_ref), (req_hbm, req_ref))
     fetches = [pltpu.make_async_copy(a, b, sems.at[i]) for i, (a, b) in enumerate(pairs_of)]
     for fetch in fetches:
         fetch.start()
-    near_terms(own_ref, left_ref, right_ref, near_ref, win, lhs, rhs, acc, list_v, list_s, pairs, sem)
+    near_terms(own_ref, pair_ref, next_ref, near_ref, win, lhs, rhs, acc, list_v, list_s, pairs, sem)
     for fetch in fetches:
         fetch.wait()
     keep_rows(table, kept_ref)
@@ -145,18 +145,22 @@
         kept_ref[first:, cols] = both.astype(BF16)
 
 
-def near_terms(own_ref, left_ref, right_ref, near_ref, win, lhs, rhs, acc, list_v, list_s, pairs, sem):
+def near_terms(own_ref, pair_ref, next_ref, near_ref, win, lhs, rhs, acc, list_v, list_s, pairs, sem):
     leaf_num = acc.shape[0] - 1
     nodes = leaf_num * LANES
     slots = list_v.shape[1]
     device = lax.axis_index("patch")
-    halo = (left_ref, own_ref, right_ref)
+    odd = device & 1
+    inner = (device > 0) & (device < lax.axis_size("patch") - 1)
+    halo = (pair_ref, own_ref, next_ref)
+    starts = ((1 - odd) * (2 * leaf_num), leaf_num, odd * (2 * leaf_num))
     leaf_of = iota((slots, LANES), 1)
     for place, ref in enumerate(halo):
         listed = ref[:, nodes:].astype(jnp.int32)
         source = listed - (device * leaf_num + 1)
-        mine = (listed > 0) & (source >= 0) & (source < leaf_num)
-        list_v[place] = jnp.where(mine, (source << 6) + (leaf_of + place * leaf_num), -1)
+        limit = leaf_num if place < 2 else jnp.where(inner, leaf_num, 0)
+        mine = (listed > 0) & (source >= 0) & (source < limit)
+        list_v[place] = jnp.where(mine, (source << 6) + (leaf_of + starts[place]), -1)
         if place == 1:
             list_v[3] = jnp.where(listed > 0, (leaf_of << 6) + (source + leaf_num), -1)
     copy = pltpu.make_async_copy(list_v, list_s, sem)
@@ -173,9 +177,9 @@
     for leaf in range(leaf_num):
         for place, ref in enumerate(halo):
             tile = ref[:, leaf * LANES : (leaf + 1) * LANES]
-            win[place * leaf_num + leaf] = tile
+            win[starts[place] + leaf] = tile
             for k, rows in enumerate(source_rows(tile)):
-                rhs[place * leaf_num + leaf, :, k * LANES : (k + 1) * LANES] = rows
+                rhs[starts[place] + leaf, :, k * LANES : (k + 1) * LANES] = rows
             if place == 1:
                 rows = target_rows(tile)
                 rows = jnp.concatenate([rows, jnp.zeros((LANES - rows.shape[0], LANES), F32)], 0)
@@ -412,8 +416,8 @@
     classes = transfer_table.shape[0]
     groups = -(-classes // GROUP)
     rows = leaf_num * width // LANES
-    up = [(i, (i + 1) % peers) for i in range(peers)]
-    down = [(j, i) for i, j in up]
+    pairs = [(i, i ^ 1) for i in range(peers)]
+    nexts = [(i, i if i in (0, peers - 1) else ((i + 1) ^ 1) - 1) for i in range(peers)]
     slots = leaf_num * far_num
     own, message = call(
         front_body,
@@ -429,8 +433,8 @@
             pltpu.SemaphoreType.DMA((4 + leaf_num // 4,)),
         ],
     )(*[held(x, pltpu.HBM) for x in (positions, densities, near_src.T, near_count[None], up_basis)])
-    left = lax.ppermute(own, "patch", up)
-    right = lax.ppermute(own, "patch", down)
+    next_own = lax.ppermute(own, "patch", nexts)
+    pair_own = lax.ppermute(own, "patch", pairs)
     message = message.reshape(peers, rows // 2, 2, LANES)
     table = lax.all_to_all(message, "patch", split_axis=0, concat_axis=0, tiled=True)
     table = table.reshape(peers * rows, LANES)
@@ -461,7 +465,7 @@
             pltpu.SemaphoreType.DMA,
             pltpu.VMEM((LANES, LANES), F32),
         ],
-    )(held(own), held(left), held(right), *[held(x, pltpu.HBM) for x in (far_count, far_slot, far_class, requests[0].T, transfer_table)])
+    )(held(own), held(pair_own), held(next_own), *[held(x, pltpu.HBM) for x in (far_count, far_slot, far_class, requests[0].T, transfer_table)])
     return call(
         far_body,
         None,

time: 50.3 us -> 47.8 us (0.950)
  the two profiles are of different devices: /device:TPU:0 before, /device:TPU:8 now
where the time goes in v8:
time: 47.8 us; the launch traced here: 47.7 us
  Pallas kernels  24.3 us (51%)
  starting transfers between devices  17.7 us (37%)
  waiting for transfers between devices  5.61 us (12%)
    pallas_call x1, Pallas kernels, per_device(): call(middle_body, [(3, nodes, F32), far_slot.shape + (jnp.int32,), (reque...  11.9 us
    all_to_all x1, starting transfers between devices, per_device(): lax.all_to_all(message, 'patch', split_axis=0, concat_axis=0, tiled=True)  10.5 us
    pallas_call x1, Pallas kernels, per_device(): call(far_body, None, 30, in_specs=[VMEM] * 7 + [HBM] * 2, out_shape=jax.S...  9.78 us
    ppermute x1, starting transfers between devices, per_device(): next_own = lax.ppermute(own, 'patch', nexts)  7.13 us
    ppermute x1, waiting for transfers between devices, per_device(): next_own = lax.ppermute(own, 'patch', nexts)  5.61 us
    pallas_call x1, Pallas kernels, per_device(): call(front_body, [(8, nodes + LANES, F32), (peers * rows, LANES, BF16)],...  2.69 us
  transfers between devices with their start and end apart: 3, of which 1 were waited for; matrix products, arithmetic and copies ran while one was open for 0% of the time, Pallas kernels for 25%

profile of v8, /device:TPU:8, one launch (start us, length us, event | category | flops | bytes accessed | tf_op | source)
XLA Modules:
  0.0 47.7 jit_solution(8859749486665511614)
XLA Ops:
  0.0 2.7 %shard_map.109 = (f32[8,2176]{1,0:T(8,128)S(1)}, bf16[2304,128]{1,0:T(8,128)(2,1)}) custom-call(f32[3,2048]{1,0:T(4,128)} %pos_hbm.1, f32[3,2048]{1,0:T(4,128)} %dens_hbm.1, s32[8,16]{1,0:T(8,128)} %bitcast.10, s32[1,16]{1,0:T(1,128)} %bitcast.12, bf16[16,144,384]{2,1,0:T(8,128)(2,1)} %up_hbm.1), custom_call_target="tpu_custom_call" | custom-call | tf_op jit(solution)/shard_map/pallas_call | solution.py:422
  2.7 10.5 %all-to-all-start = ((bf16[128,9,2,128]{3,2,1,0:T(2,128)(2,1)}), bf16[128,9,2,128]{3,2,1,0:T(2,128)(2,1)S(1)}, u32[]{:S(2)}, u32[]{:S(2)}) async-start(bf16[128,9,2,128]{3,2,1,0:T(2,128)(2,1)} %bitcast.2), calls=%async_computation | async-start | bytes 1179648 | tf_op jit(solution)/shard_map/all_to_all | solution.py:439
  13.2 7.1 %collective-permute-start.1 = (f32[8,2176]{1,0:T(8,128)S(1)}, f32[8,2176]{1,0:T(8,128)S(1)}, u32[]{:S(2)}, u32[]{:S(2)}) collective-permute-start(f32[8,2176]{1,0:T(8,128)S(1)} %get-tuple-element.13.own_ref), channel_id=1, source_target_pairs={{0,0},{1,2},{2,1},{3,4},{4,3},{5,6},{6,5},{7,8},{8,7},{9,10},{10,9... | collective-permute-start | bytes 208904 | tf_op jit(solution)/shard_map/ppermute | solution.py:436
  20.3 0.1 collective-permute-start
  20.4 5.6 %collective-permute-done.1.next_ref = f32[8,2176]{1,0:T(8,128)S(1)} collective-permute-done((f32[8,2176]{1,0:T(8,128)S(1)}, f32[8,2176]{1,0:T(8,128)S(1)}, u32[]{:S(2)}, u32[]{:S(2)}) %collective-permute-start.1) | collective-permute-done | bytes 69664 | tf_op jit(solution)/shard_map/ppermute | solution.py:436
  26.0 0.0 collective-permute-done.pair_ref
  26.0 11.9 %shard_map.110 = (f32[3,2048]{1,0:T(4,128)S(1)}, s32[16,32]{1,0:T(8,128)S(1)}, s32[4,128]{1,0:T(4,128)S(1)}, bf16[512,128]{1,0:T(8,128)(2,1)S(1)}, bf16[48,20736]{1,0:T(8,128)(2,1)S(1)}) custom-call(f32[8,2176]{1,0:T(8,128)S(1)} %get-tuple-element.13.own_ref, f32[8,2176]{1,0:T(8,128)S(1)} %collective-permute-done.pair_ref, ...), custom_call_target="tpu_custom_call" | custom-call | tf_op jit(solution)/shard_map/pallas_call | solution.py:442
  37.9 0.0 all-to-all-done
  37.9 9.8 %shard_map.111 = f32[3,2048]{1,0:T(4,128)} custom-call(bf16[2304,128]{1,0:T(8,128)(2,1)S(1)} %bitcast.8, s32[16,32]{1,0:T(8,128)S(1)} %get-tuple-element.14.slot_ref, s32[4,128]{1,0:T(4,128)S(1)} %get-tuple-element.15.req_ref, bf16[512,128]{1,0:T(8,128)(2,1)S(1)} %get-tuple-element.16.kind_ref, bf16[48,20736]{1,0:T(8,128)(2,1)S(1)} %get-tuple-element.17.kept_ref, ...), custom_call_target="tpu_custom_call" | custom-call | tf_op jit(solution)/shard_map/pallas_call | solution.py:469
Async XLA Ops:
  2.7 35.2 %all-to-all-start = ((bf16[128,9,2,128]{3,2,1,0:T(2,128)(2,1)}), bf16[128,9,2,128]{3,2,1,0:T(2,128)(2,1)S(1)}, u32[]{:S(2)}, u32[]{:S(2)}) async-start(bf16[128,9,2,128]{3,2,1,0:T(2,128)(2,1)} %bitcast.2), calls=%async_computation | async-start | bytes 1179648 | tf_op jit(solution)/shard_map/all_to_all | solution.py:439
  13.2 12.8 %collective-permute-start.1 = (f32[8,2176]{1,0:T(8,128)S(1)}, f32[8,2176]{1,0:T(8,128)S(1)}, u32[]{:S(2)}, u32[]{:S(2)}) collective-permute-start(f32[8,2176]{1,0:T(8,128)S(1)} %get-tuple-element.13.own_ref), channel_id=1, source_target_pairs={{0,0},{1,2},{2,1},{3,4},{4,3},{5,6},{6,5},{7,8},{8,7},{9,10},{10,9... | collective-permute-start | bytes 208904 | tf_op jit(solution)/shard_map/ppermute | solution.py:436
  20.3 5.7 %collective-permute-start = (f32[8,2176]{1,0:T(8,128)S(1)}, f32[8,2176]{1,0:T(8,128)S(1)}, u32[]{:S(2)}, u32[]{:S(2)}) collective-permute-start(f32[8,2176]{1,0:T(8,128)S(1)} %get-tuple-element.13.own_ref), channel_id=1, source_target_pairs={{0,1},{1,0},{2,3},{3,2},{4,5},{5,4},{6,7},{7,6},{8,9},{9,8},{10,11... | collective-permute-start | bytes 208904 | tf_op jit(solution)/shard_map/ppermute | solution.py:437
